TPU v7x, 32 devices: a whole 2x2x4 slice. The times are simulated.
32 devices in a mesh: pb: 2 (over core), row: 4 (over y, x), col: 4 (over z).
Axes of the slice: x: 2, y: 2, z: 4, core: 2. Of those that a mesh axis runs over, the one named last changes fastest.
Arguments:
- chol: bfloat16 [64, 1344, 1344], P('pb', 'row', 'col'), may hold values from -0.29882812 to 0.29882812
- amplitudes: bfloat16 [144, 1200], P(None, 'row'), may hold values from -0.59765625 to 0.59765625
Outputs:
- dressed: bfloat16 [64, 1344, 1344], P(('pb', 'row', 'col'))
- fock: float32 [1344, 1344], P('row', 'col')
All inputs are finite; a program needn't handle non-finite values.
Results may differ from a plain program's by a relative error of at most 0.02.
Values may be sent and summed in bfloat16 or wider, within the bound.
A program may use at most 128 MiB of HBM per device.

v0:
```python
import functools
import jax
import numpy as np
import jax.numpy as jnp
from jax import lax
from jax.experimental import pallas as pl
from jax.experimental.pallas import tpu as pltpu
from jax.sharding import PartitionSpec as P

OG = 9
VG = 75
SH = 84
MESH = pl.DeviceIdType.MESH


def peer(index, mode, size):
    if size & (size - 1):
        return lax.rem(index + mode, size)
    bits = [1 << k for k in range(size.bit_length() - 1)]
    return sum(lax.rem(lax.rem(lax.div(index, bit), 2) + mode // bit % 2, 2) * bit for bit in bits)


def lanes(parts):
    return jnp.concatenate([p.astype(jnp.float32) for p in parts], axis=1).astype(jnp.bfloat16)


def pack(a, b, mid, low, rows):
    first, second = a.astype(jnp.float32), b.astype(jnp.float32)
    wide = jnp.concatenate([first[:, :mid], second[:, :mid]], axis=1).astype(jnp.bfloat16)
    thin = jnp.concatenate([first[:, mid:], second[:, mid:]], axis=0)
    pieces = [thin[k * rows : (k + 1) * rows] for k in range(thin.shape[0] // rows)]
    pieces.append(jnp.zeros((rows, 128 - low * len(pieces)), jnp.float32))
    return wide, jnp.concatenate(pieces, axis=1).astype(jnp.bfloat16)


def unpack_tail(wide, thin, which, mid, low, rw):
    wide = wide.astype(jnp.float32)[:, which * mid : (which + 1) * mid]
    thin = thin.astype(jnp.float32)
    rows = thin.shape[0]
    pieces = [thin[:, k * low : (k + 1) * low] for k in range(2 * rw // rows)]
    thin = jnp.concatenate(pieces, axis=0)[which * rw : (which + 1) * rw]
    return jnp.concatenate([wide, thin], axis=1)


def dress(R, C, n, mains, tail, amps, pick, pick_t, primed, cols, put_dressed, put_fock):
    rw = mains.shape[1]
    th = rw * n
    for j in range(C):
        shift = None
        for i in range(C):
            pieces = []
            for m in range(n):
                s = (i * n + m) * C + j
                pieces.append(jnp.concatenate([mains[s], tail[s]], axis=1))
            tile = pieces[0]
            if n > 1:
                tile = jnp.concatenate([p.astype(jnp.float32) for p in pieces], axis=0).astype(jnp.bfloat16)
            primed[i, j] = tile
            term = jnp.dot(amps[i], tile, preferred_element_type=jnp.float32)
            term = term.astype(jnp.bfloat16).astype(jnp.float32)
            shift = term if shift is None else shift + term
        hi = shift.astype(jnp.bfloat16)
        lo = (shift - hi.astype(jnp.float32)).astype(jnp.bfloat16)
        for i in range(C):
            placed = jnp.dot(pick[i], hi, preferred_element_type=jnp.float32)
            placed = placed + jnp.dot(pick[i], lo, preferred_element_type=jnp.float32)
            primed[i, j] = (primed[i, j].astype(jnp.float32) - placed).astype(jnp.bfloat16)
    weight = jnp.zeros((1, 1), jnp.float32)
    for i in range(C):
        occ = None
        for j in range(C):
            part = jnp.dot(primed[i, j], pick[j], preferred_element_type=jnp.float32)
            occ = part if occ is None else occ + part
        cols[i] = occ.astype(jnp.bfloat16)
        diag = occ * pick[i].astype(jnp.float32)
        weight = weight + jnp.sum(jnp.sum(diag, axis=1, keepdims=True), axis=0, keepdims=True)
    for i in range(C):
        strip = []
        for j in range(C):
            extra = jnp.dot(cols[i], amps[j], preferred_element_type=jnp.float32)
            tile = (primed[i, j].astype(jnp.float32) + extra).astype(jnp.bfloat16)
            primed[i, j] = tile
            strip.append(tile)
        put_dressed(i, lanes(strip))
    for j in range(C):
        rows = None
        for i in range(C):
            part = jnp.dot(pick_t[i], primed[i, j], preferred_element_type=jnp.float32)
            rows = part if rows is None else rows + part
        rows = rows.astype(jnp.bfloat16)
        for i in range(C):
            swapped = jnp.dot(cols[i], rows, preferred_element_type=jnp.float32)
            put_fock(i, j, 2.0 * weight * primed[i, j].astype(jnp.float32) - swapped)


def exchange_kernel(
    R, C, n, mid, low, rows, chol, amp, widen, pick, pick_t,
    main_b, wide_all, thin_all, tail_b, amps, dressed, fock,
    tails, wide_out, thin_out, own, amp_out, amp_all, mains, tail_a, wides, thins, primed, cols,
    send, recv, lsem,
):
    r = lax.axis_index("row")
    c = lax.axis_index("col")
    me = r * C + c
    rw = chol.shape[1]
    full = mains.shape[2]
    tail_in = pltpu.make_async_copy(chol.at[:, :, pl.ds(full, mid + low)], tails, lsem.at[0])
    tail_in.start()
    own_in = pltpu.make_async_copy(chol.at[pl.ds(me * 2, 2), :, pl.ds(0, full)], own, lsem.at[1])
    own_in.start()
    peers = [(dr, dc) for dr in range(R) for dc in range(C) if (dr, dc) != (0, 0)]
    far = [t for t in peers if t[1] >= C // 2]
    near = [t for t in peers if t[1] < C // 2]
    mixed = [t for pair in zip(far, near) for t in pair]
    peers = mixed + [t for t in far + near if t not in mixed]
    barrier = pltpu.get_barrier_semaphore()
    for dr, dc in peers:
        pl.semaphore_signal(
            barrier, inc=1, device_id={"row": peer(r, dr, R), "col": peer(c, dc, C)}, device_id_type=MESH
        )
    wide_amp = jnp.dot(amp[...], widen[...], preferred_element_type=jnp.float32).astype(jnp.bfloat16)
    amp_out[...] = wide_amp
    pl.semaphore_wait(barrier, len(peers))

    def move(kind, src, dst, dr, dc):
        return pltpu.make_async_remote_copy(
            src_ref=src,
            dst_ref=dst,
            send_sem=send.at[kind, dr * C + dc],
            recv_sem=recv.at[kind, dr * C + dc],
            device_id={"row": peer(r, dr, R), "col": peer(c, dc, C)},
            device_id_type=MESH,
        )

    first, second = [], []
    for dr, dc in peers:
        to = peer(r, dr, R) * C + peer(c, dc, C)
        first.append(move(1, chol.at[to * 2, :, pl.ds(0, full)], mains.at[me], dr, dc))
        first[-1].start()
    amp_moves = [move(0, amp_out, amp_all.at[r], dr, 0) for dr in range(1, R)]
    for copy in amp_moves:
        copy.start()
    amp_all[r] = wide_amp
    tail_in.wait()

    def pack_one(d, carry):
        wide, thin = pack(tails[2 * d], tails[2 * d + 1], mid, low, rows)
        wide_out[d] = wide
        thin_out[d] = thin
        return carry

    lax.fori_loop(0, R * C, pack_one, 0)
    for dr, dc in peers:
        to = peer(r, dr, R) * C + peer(c, dc, C)
        first.append(move(2, wide_out.at[to], wide_all.at[me], dr, dc))
        first.append(move(3, thin_out.at[to], thin_all.at[me], dr, dc))
        first[-2].start()
        first[-1].start()
    for dr, dc in peers:
        to = peer(r, dr, R) * C + peer(c, dc, C)
        second.append(move(4, chol.at[to * 2 + 1, :, pl.ds(0, full)], main_b.at[me], dr, dc))
        second[-1].start()
    own_in.wait()
    mains[me] = own[0]
    local = [
        pltpu.make_async_copy(own.at[1], main_b.at[me], lsem.at[3]),
        pltpu.make_async_copy(wide_out.at[me], wide_all.at[me], lsem.at[4]),
        pltpu.make_async_copy(thin_out.at[me], thin_all.at[me], lsem.at[5]),
    ]
    for copy in local:
        copy.start()
    for copy in amp_moves:
        copy.wait()
    for i in range(C):
        amps[i] = amp_all[i] if n == 1 else lanes([amp_all[i * n + m] for m in range(n)])
    for copy in local:
        copy.wait()
    for copy in first:
        copy.wait()
    loads = [
        pltpu.make_async_copy(wide_all, wides, lsem.at[6]),
        pltpu.make_async_copy(thin_all, thins, lsem.at[7]),
    ]
    for copy in loads:
        copy.start()
    for copy in loads:
        copy.wait()
    th = rw * n

    def open_tail(s, carry):
        tail_a[s] = unpack_tail(wides[s], thins[s], 0, mid, low, rw).astype(jnp.bfloat16)
        tail_b[s] = unpack_tail(wides[s], thins[s], 1, mid, low, rw).astype(jnp.bfloat16)
        return carry

    lax.fori_loop(0, R * C, open_tail, 0)

    def put_dressed(i, strip):
        dressed[0, pl.ds(i * th, th), :] = strip

    def put_fock(i, j, value):
        fock[i, j] = value

    dress(R, C, n, mains, tail_a, amps, pick, pick_t, primed, cols, put_dressed, put_fock)
    for copy in second:
        copy.wait()


def dress_kernel(
    R, C, n, B, mains, tail, amps, pick, pick_t, before, before_fock,
    dressed, fock, primed, cols, held, result, partial, sem,
):
    share = C // B
    th = mains.shape[1] * n
    load = pltpu.make_async_copy(before, held, sem.at[0])
    load.start()
    load_fock = pltpu.make_async_copy(before_fock, partial, sem.at[1])
    load_fock.start()
    store = pltpu.make_async_copy(held, dressed.at[pl.ds(0, 1)], sem.at[2])
    final = pltpu.make_async_copy(result, dressed.at[pl.ds(1, 1)], sem.at[3])

    def put_dressed(i, strip):
        if i == 0:
            load.wait()
            store.start()
        result[0, pl.ds(i * th, th), :] = strip
        if i == C - 1:
            load_fock.wait()
            final.start()

    def put_fock(i, j, value):
        fock[j // share, i, j % share] = (partial[i, j] + value).astype(jnp.bfloat16)

    dress(R, C, n, mains, tail, amps, pick, pick_t, primed, cols, put_dressed, put_fock)
    store.wait()
    final.wait()


def reduce_kernel(B, R, C, part, out, got1, half, got2, block, got3, s1, r1, s2, r2, s3, r3, s4, r4):
    b = lax.axis_index("pb")
    r = lax.axis_index("row")
    c = lax.axis_index("col")
    share = C // B
    barrier = pltpu.get_barrier_semaphore()
    for axis, index, size in (("pb", b, B), ("row", r, R), ("col", c, C)):
        for d in range(1, size):
            pl.semaphore_signal(barrier, inc=1, device_id={axis: lax.rem(index + d, size)}, device_id_type=MESH)
    pl.semaphore_wait(barrier, B + R + C - 3)
    order = list(range(1, R)) + [0]

    def to_half(k, d, e):
        to, row = lax.rem(b + e, B), lax.rem(r + d, R)
        return pltpu.make_async_remote_copy(
            src_ref=part.at[to, row, k], dst_ref=got1.at[e - 1, k, d],
            send_sem=s1.at[e, k, d], recv_sem=r1.at[e, k, d],
            device_id={"pb": to}, device_id_type=MESH,
        )

    def to_row(k, d):
        return pltpu.make_async_remote_copy(
            src_ref=half.at[k, d], dst_ref=got2.at[k, d], send_sem=s2.at[k, d], recv_sem=r2.at[k, d],
            device_id={"row": lax.rem(r + d, R)}, device_id_type=MESH,
        )

    def to_col(k, d):
        return pltpu.make_async_remote_copy(
            src_ref=block.at[k], dst_ref=got3.at[d - 1], send_sem=s3.at[k], recv_sem=r3.at[d],
            device_id={"col": b * share + k}, device_id_type=MESH,
        )

    for k in range(share):
        for d in order:
            for e in range(1, B):
                to_half(k, d, e).start()
    for k in range(share):
        for d in order:
            value = part[b, lax.rem(r + d, R), k].astype(jnp.float32)
            for e in range(1, B):
                to_half(k, d, e).wait()
                value = value + got1[e - 1, k, d].astype(jnp.float32)
            half[k, d] = value.astype(jnp.bfloat16)
            if d:
                to_row(k, d).start()
    for k in range(share):
        value = half[k, 0].astype(jnp.float32)
        for d in range(1, R):
            to_row(k, d).wait()
            value = value + got2[k, d].astype(jnp.float32)
        block[k] = value.astype(jnp.bfloat16)
        for d in range(1, C):
            @pl.when(lax.rem(c + d, C) == b * share + k)
            def _():
                to_col(k, d).start()

    for k in range(share):
        @pl.when(c == b * share + k)
        def _():
            total = block[k].astype(jnp.float32)
            for d in range(1, C):
                to_col(k, d).wait_recv()
                total = total + got3[d - 1].astype(jnp.float32)
            out[...] = total

    def to_pb(d):
        return pltpu.make_async_remote_copy(
            src_ref=out, dst_ref=out, send_sem=s4.at[d], recv_sem=r4.at[0],
            device_id={"pb": lax.rem(b + d, B)}, device_id_type=MESH,
        )

    mine = c // share == b

    @pl.when(mine)
    def _():
        for d in range(1, B):
            to_pb(d).start()
        for d in range(1, B):
            to_pb(d).wait_send()

    @pl.when(jnp.logical_not(mine))
    def _():
        to_pb(1).wait_recv()

    for k in range(share):
        @pl.when(c != b * share + k)
        def _():
            to_col(k, 1).wait_send()


def local(chol, amplitudes):
    B, R, C = lax.axis_size("pb"), lax.axis_size("row"), lax.axis_size("col")
    q_local, rw, cw = chol.shape
    n = cw // rw
    norb = C * cw
    occ = amplitudes.shape[0]
    groups = rw // SH
    full = cw // 128 * 128
    mid = 64
    low = cw - full - mid
    rows = 2 * rw // 7
    share = C // B
    virtual = np.arange(groups * VG)
    widen = virtual[:, None] // VG * SH + OG + virtual[:, None] % VG == np.arange(rw)[None, :]
    widen = jnp.asarray(widen, jnp.bfloat16)
    index = np.arange(occ)
    place = np.arange(norb)[:, None] == (index // OG * SH + index % OG)[None, :]
    place = place.reshape(C, cw, occ)
    pick = jnp.asarray(place, jnp.bfloat16)
    pick_t = jnp.asarray(place.transpose(0, 2, 1), jnp.bfloat16)
    hbm = pl.BlockSpec(memory_space=pl.ANY)
    vmem = pl.BlockSpec(memory_space=pltpu.VMEM)
    dma = pltpu.SemaphoreType.DMA
    bf16 = lambda *shape: pltpu.VMEM(shape, jnp.bfloat16)
    shape = lambda *dims: jax.ShapeDtypeStruct(dims, jnp.bfloat16)
    limit = 60 * 1024 * 1024
    N = R * C
    main_b, wide_all, thin_all, tail_b, amps, before, before_fock = pl.pallas_call(
        functools.partial(exchange_kernel, R, C, n, mid, low, rows),
        out_shape=(
            shape(N, rw, full),
            shape(N, rw, 128),
            shape(N, rows, 128),
            shape(N, rw, mid + low),
            shape(C, occ, cw),
            shape(1, norb, norb),
            jax.ShapeDtypeStruct((C, C, cw, cw), jnp.float32),
        ),
        in_specs=[hbm, vmem, vmem, vmem, vmem],
        out_specs=(hbm, hbm, hbm, vmem, vmem, vmem, vmem),
        scratch_shapes=[
            bf16(q_local, rw, mid + low),
            bf16(N, rw, 128),
            bf16(N, rows, 128),
            bf16(2, rw, full),
            bf16(occ, rw),
            bf16(R, occ, rw),
            bf16(N, rw, full),
            bf16(N, rw, mid + low),
            bf16(N, rw, 128),
            bf16(N, rows, 128),
            bf16(C, C, cw, cw),
            bf16(C, cw, occ),
            dma((5, N)),
            dma((5, N)),
            dma((8,)),
        ],
        compiler_params=pltpu.CompilerParams(collective_id=0, has_side_effects=True, vmem_limit_bytes=limit),
        name="exchange",
    )(chol, amplitudes, widen, pick, pick_t)
    dressed, fock = pl.pallas_call(
        functools.partial(dress_kernel, R, C, n, B),
        out_shape=(shape(2, norb, norb), shape(B, C, share, cw, cw)),
        in_specs=[vmem] * 5 + [hbm, hbm],
        out_specs=(hbm, vmem),
        scratch_shapes=[
            bf16(C, C, cw, cw),
            bf16(C, cw, occ),
            bf16(1, norb, norb),
            bf16(1, norb, norb),
            pltpu.VMEM((C, C, cw, cw), jnp.float32),
            dma((4,)),
        ],
        compiler_params=pltpu.CompilerParams(vmem_limit_bytes=limit),
        name="dress",
    )(main_b, tail_b, amps, pick, pick_t, before, before_fock)
    part = fock
    if n > 1:
        part = jnp.transpose(fock.reshape(B, C, share, n, rw, cw), (0, 1, 3, 2, 4, 5)).reshape(B, R, share, rw, cw)
    out = pl.pallas_call(
        functools.partial(reduce_kernel, B, R, C),
        out_shape=jax.ShapeDtypeStruct((rw, cw), jnp.float32),
        in_specs=[vmem],
        out_specs=vmem,
        scratch_shapes=[
            bf16(B - 1, share, R, rw, cw),
            bf16(share, R, rw, cw),
            bf16(share, R, rw, cw),
            bf16(share, rw, cw),
            bf16(C - 1, rw, cw),
            dma((B, share, R)), dma((B, share, R)), dma((share, R)), dma((share, R)),
            dma((share,)), dma((C,)), dma((B,)), dma((1,)),
        ],
        compiler_params=pltpu.CompilerParams(collective_id=1, has_side_effects=True, vmem_limit_bytes=limit),
        name="reduce",
    )(part)
    return dressed, out


def solution(mesh):
    return jax.shard_map(
        local,
        mesh=mesh,
        in_specs=(P("pb", "row", "col"), P(None, "row")),
        out_specs=(P(("pb", "row", "col"), None, None), P("row", "col")),
        check_vma=False,
    )
```

profile of v0, /device:TPU:1, one launch (start us, length us, event | category | flops | bytes accessed | tf_op | source)
XLA Modules:
  0.0 228.0 jit_solution(13651042709310187534)
XLA Ops:
  0.6 169.5 %exchange.1 = (bf16[16,336,256]{2,1,0:T(8,128)(2,1)}, bf16[16,336,128]{2,1,0:T(8,128)(2,1)}, bf16[16,96,128]{2,1,0:T(8,128)(2,1)}, bf16[16,336,80]{2,1,0:T(8,128...) custom-call(bf16[32,336,336]{2,1,0:T(8,128)(2,1)} %chol.1, ...), custom_call_target="tpu_custom_call" | custom-call | tf_op jit(solution)/shard_map/exchange/pallas_call | solution.py:355
  170.2 16.3 %dress.1 = (bf16[2,1344,1344]{2,1,0:T(8,128)(2,1)}, bf16[2,4,2,336,336]{4,3,2,1,0:T(8,128)(2,1)}) custom-call(bf16[16,336,256]{2,1,0:T(8,128)(2,1)} %get-tuple-element.9.mains, bf16[16,336,80]{2,1,0:T(8,128)(2,1)} %get-tuple-element.10.tail, bf16[4,144,336]{2,1,0:T(8,128)(2,1)} %get-tuple-element.11.amps, bf16[4,336,144]{2,1,0:T(8,128)(2,1)} %constant.7.clone.pick, ...), custom_call_target="tpu_custom_call" | custom-call | tf_op jit(solution)/shard_map/dress/pallas_call | solution.py:388
  186.5 39.6 %reduce.1 = f32[336,336]{1,0:T(8,128)} custom-call(bf16[2,4,2,336,336]{4,3,2,1,0:T(8,128)(2,1)} %get-tuple-element.15.part), custom_call_target="tpu_custom_call" | custom-call | tf_op jit(solution)/shard_map/reduce/pallas_call | solution.py:407
  226.1 1.9 copy.8
where the time goes:
time: 232 us; the launch traced here: 228 us
  Pallas kernels  225 us (97%)
    pallas_call x1, Pallas kernels, local(): pl.pallas_call(functools.partial(exchange_kernel, R, C, n, mid, low, rows...  170 us
    pallas_call x1, Pallas kernels, local(): pl.pallas_call(functools.partial(reduce_kernel, B, R, C), out_shape=jax.S...  39.6 us
    pallas_call x1, Pallas kernels, local(): pl.pallas_call(functools.partial(dress_kernel, R, C, n, B), out_shape=(sh...  16.3 us

commit v1 on v0

v1 whole, which is shorter than its diff:
```python
import functools
import jax
import numpy as np
import jax.numpy as jnp
from jax import lax
from jax.experimental import pallas as pl
from jax.experimental.pallas import tpu as pltpu
from jax.sharding import PartitionSpec as P

OG = 9
VG = 75
SH = 84
LANE = 128
MESH = pl.DeviceIdType.MESH
f32, bf16 = jnp.float32, jnp.bfloat16


def dot(a, b):
    return jnp.dot(a, b, preferred_element_type=f32)


def peer(index, mode, size):
    if size & (size - 1):
        return lax.rem(index + mode, size)
    bits = [1 << k for k in range(size.bit_length() - 1)]
    flip = lambda bit: lax.rem(lax.rem(lax.div(index, bit), 2) + lax.rem(lax.div(mode, bit), 2), 2) * bit
    return sum(flip(bit) for bit in bits)


def lanes(parts):
    return jnp.concatenate([p.astype(f32) for p in parts], axis=1).astype(bf16)


def pack(first, second, mid, low, rows):
    wide = jnp.concatenate([first[:, :mid], second[:, :mid]], axis=1).astype(bf16)
    thin = jnp.concatenate([first[:, mid:], second[:, mid:]], axis=0)
    pieces = [thin[k * rows : (k + 1) * rows] for k in range(thin.shape[0] // rows)]
    pieces.append(jnp.zeros((rows, LANE - low * len(pieces)), f32))
    return wide, jnp.concatenate(pieces, axis=1).astype(bf16)


def unpack(wide, thin, mid, low, rw):
    wide, thin = wide.astype(f32), thin.astype(f32)
    rows = thin.shape[0]
    pieces = [thin[:, k * low : (k + 1) * low] for k in range(2 * rw // rows)]
    thin = jnp.concatenate(pieces, axis=0)
    blank = jnp.zeros((rw, LANE - mid - low), f32)
    for v in range(2):
        part = [wide[:, v * mid : (v + 1) * mid], thin[v * rw : (v + 1) * rw], blank]
        yield jnp.concatenate(part, axis=1).astype(bf16)


SLOTS = 4
A_MAIN, WIDE, THIN, B_FIRST, B_LAST = range(5)


def main_kernel(
    B, R, C, n, mid, low, rows, chol, amp, widen, perm, back, pick, pick_t, occ_of,
    dressed, fock,
    stage, packed, wide_out, thin_out, wides, thins, x, d, total, amp_out, amp_all, amps, amp_perm, cols,
    part, got1, half, got2, block, got3, final, strips,
    send, recv, amp_send, amp_recv, load, s1, r1, s2, r2, s3, r3, s4, r4, out_sem,
):
    b, r, c = lax.axis_index("pb"), lax.axis_index("row"), lax.axis_index("col")
    me = r * C + c
    N = R * C
    share = C // B
    rw, cw = chol.shape[1], chol.shape[2]
    th = rw * n
    near = lax.div(c, share)

    def place(m):
        k = lax.rem(lax.div(m, 2) + lax.rem(m, 2), N // 2)
        dc = lax.rem(k, C // 2) + (C // 2) * (1 - lax.rem(m, 2))
        return peer(r, lax.div(k, C // 2), R), peer(c, dc, C)

    def fetch(m):
        row, col = place(m)
        slot = lax.rem(m, SLOTS)
        return pltpu.make_async_copy(chol.at[pl.ds((row * C + col) * 2, 2)], stage.at[slot], load.at[slot])

    for m in range(SLOTS):
        fetch(m).start()
    barrier = pltpu.get_barrier_semaphore()
    for m in range(N - 1):
        row, col = place(m)
        pl.semaphore_signal(barrier, inc=1, device_id={"row": row, "col": col}, device_id_type=MESH)
    for e in range(1, B):
        pl.semaphore_signal(barrier, inc=1, device_id={"pb": lax.rem(b + e, B)}, device_id_type=MESH)
    own_amp = dot(amp[...], widen[...]).astype(bf16)
    amp_out[...] = own_amp
    amp_all[r] = own_amp
    pl.semaphore_wait(barrier, N - 1 + B - 1)

    def move(kind, m, src_rank):
        row, col = place(m)
        from_row, from_col = lax.div(src_rank, C), lax.rem(src_rank, C)
        src, dst = {
            A_MAIN: (packed.at[m, 0], x.at[0, pl.ds(0, 2), from_col, from_row]),
            WIDE: (wide_out.at[m], wides.at[src_rank]),
            THIN: (thin_out.at[m], thins.at[src_rank]),
            B_FIRST: (packed.at[m, 1, 0], x.at[1, 0, from_col, from_row]),
            B_LAST: (packed.at[m, 1, 1], x.at[1, 1, from_col, from_row]),
        }[kind]
        return pltpu.make_async_remote_copy(
            src_ref=src, dst_ref=dst, send_sem=send.at[kind, m], recv_sem=recv.at[kind, src_rank],
            device_id={"row": row, "col": col}, device_id_type=MESH,
        )

    def permute(m, carry):
        fetch(m).wait()
        slot = lax.rem(m, SLOTS)
        tails = []
        for v in range(2):
            y = dot(stage[slot, v], perm[...])
            packed[m, v, 0] = y[:, :LANE].astype(bf16)
            packed[m, v, 1] = y[:, LANE : 2 * LANE].astype(bf16)
            tails.append(y[:, 2 * LANE : 2 * LANE + mid + low])

        @pl.when(m < N - 1)
        def _():
            move(A_MAIN, m, me).start()

        wide, thin = pack(tails[0], tails[1], mid, low, rows)
        wide_out[m] = wide
        thin_out[m] = thin

        @pl.when(m + SLOTS < N)
        def _():
            fetch(m + SLOTS).start()

        return carry

    lax.fori_loop(0, N, permute, 0)

    def amp_move(to, src):
        return pltpu.make_async_remote_copy(
            src_ref=amp_out, dst_ref=amp_all.at[src], send_sem=amp_send.at[to], recv_sem=amp_recv.at[src],
            device_id={"row": to}, device_id_type=MESH,
        )

    others = [peer(r, k, R) for k in range(1, R)]
    for to in others:
        amp_move(to, r).start()

    def start_all(kinds):
        def one(m, carry):
            for kind in kinds:
                move(kind, m, me).start()
            return carry

        lax.fori_loop(0, N - 1, one, 0)

    start_all((WIDE, THIN))
    start_all((B_FIRST,))
    start_all((B_LAST,))
    for v in range(2):
        for k in range(2):
            x[v, k, c, r] = packed[N - 1, v, k]
    wides[me] = wide_out[N - 1]
    thins[me] = thin_out[N - 1]

    def wait_from(kinds, rank):
        @pl.when(rank != me)
        def _():
            for kind in kinds:
                move(kind, 0, rank).wait_recv()

    def wait_all(kinds):
        def one(s, carry):
            wait_from(kinds, s)
            return carry

        lax.fori_loop(0, N, one, 0)

    for src in others:
        amp_move(src, src).wait_recv()
    for i in range(C):
        whole = amp_all[i] if n == 1 else lanes([amp_all[i * n + m] for m in range(n)])
        amps[i] = whole
        ordered = dot(whole, perm[...]).astype(bf16)
        for k in range(3):
            amp_perm[k, i] = ordered[:, k * LANE : (k + 1) * LANE]

    def side(ref, h):
        return jnp.concatenate([ref[h * share + s] for s in range(share)], axis=1)

    def arrived(v, k, h, i):
        if n == 1:
            return side(x.at[v, k, :, i], h)
        tall = [side(x.at[v, k, :, i * n + m], h).astype(f32) for m in range(n)]
        return jnp.concatenate(tall, axis=0).astype(bf16)

    def prime(v, k, h):
        def add(i, shift):
            return shift + dot(amps[i], arrived(v, k, h, i)).astype(bf16).astype(f32)

        shift = lax.fori_loop(0, C, add, jnp.zeros((amps.shape[1], share * LANE), f32))
        hi = shift.astype(bf16)
        lo = (shift - hi.astype(f32)).astype(bf16)

        def take(i, carry):
            placed = dot(pick[i], hi) + dot(pick[i], lo)
            value = (arrived(v, k, h, i).astype(f32) - placed).astype(bf16)
            for s in range(share):
                d[v, k, h * share + s, i] = value[:, s * LANE : (s + 1) * LANE]
            return carry

        lax.fori_loop(0, C, take, 0)

    def occupied(v):
        def one(i, weight):
            occ = sum(dot(side(d.at[v, 0, :, i], h), occ_of[h]) for h in range(B))
            cols[v, i] = occ.astype(bf16)
            diag = occ * pick[i].astype(f32)
            return weight + jnp.sum(jnp.sum(diag, axis=1, keepdims=True), axis=0, keepdims=True)

        return lax.fori_loop(0, C, one, jnp.zeros((1, 1), f32))

    def dress(v, k, h, weight):
        amp_side = side(amp_perm.at[k], h)

        def add(i, occ_rows):
            value = (side(d.at[v, k, :, i], h).astype(f32) + dot(cols[v, i], amp_side)).astype(bf16)
            for s in range(share):
                d[v, k, h * share + s, i] = value[:, s * LANE : (s + 1) * LANE]
            return occ_rows + dot(pick_t[i], value)

        occ_rows = lax.fori_loop(0, C, add, jnp.zeros((amps.shape[1], share * LANE), f32)).astype(bf16)

        def put(i, carry):
            value = 2.0 * weight * side(d.at[v, k, :, i], h).astype(f32) - dot(cols[v, i], occ_rows)
            for s in range(share):
                mine = value[:, s * LANE : (s + 1) * LANE]
                if v == 0:
                    total[k, h * share + s, i] = mine
                else:
                    mine = total[k, h * share + s, i] + mine
                    for m in range(n):
                        part[k, h, i * n + m, s] = mine[m * rw : (m + 1) * rw].astype(bf16)
            return carry

        lax.fori_loop(0, C, put, 0)

    def put_out(v, i):
        return pltpu.make_async_copy(strips.at[i], dressed.at[v, pl.ds(i * th, th), :], out_sem.at[i])

    def unpermute(v):
        def one(i, carry):
            natural = []
            for j in range(C):
                ordered = jnp.concatenate([d[v, k, j, i] for k in range(3)], axis=1)
                natural.append(dot(ordered, back[...]))
            strips[i] = jnp.concatenate(natural, axis=1).astype(bf16)
            put_out(v, i).start()
            return carry

        lax.fori_loop(0, C, one, 0)

    wait_all((A_MAIN,))
    wait_all((WIDE, THIN))

    def open_tail(s, carry):
        row, col = lax.div(s, C), lax.rem(s, C)
        for v, value in enumerate(unpack(wides[s], thins[s], mid, low, rw)):
            x[v, 2, col, row] = value
        return carry

    lax.fori_loop(0, N, open_tail, 0)

    def prime_a(t, carry):
        prime(0, lax.div(t, B), lax.rem(t, B))
        return carry

    lax.fori_loop(0, 3 * B, prime_a, 0)
    weight_a = occupied(0)

    def dress_a(t, carry):
        dress(0, lax.div(t, B), lax.rem(t, B), weight_a)
        return carry

    lax.fori_loop(0, 3 * B, dress_a, 0)
    unpermute(0)

    def to_half(k, h, e):
        return pltpu.make_async_remote_copy(
            src_ref=part.at[k, h], dst_ref=got1.at[k, e - 1], send_sem=s1.at[k, e], recv_sem=r1.at[k, e],
            device_id={"pb": h}, device_id_type=MESH,
        )

    def to_row(k, e):
        return pltpu.make_async_remote_copy(
            src_ref=half.at[k, e], dst_ref=got2.at[k, e], send_sem=s2.at[k, e], recv_sem=r2.at[k, e],
            device_id={"row": lax.rem(r + e, R)}, device_id_type=MESH,
        )

    def to_col(k, s, src):
        return pltpu.make_async_remote_copy(
            src_ref=block.at[k, s], dst_ref=got3.at[k, src], send_sem=s3.at[k, s], recv_sem=r3.at[k, src],
            device_id={"col": b * share + s}, device_id_type=MESH,
        )

    def to_pb(k, e):
        return pltpu.make_async_remote_copy(
            src_ref=final.at[k], dst_ref=final.at[k], send_sem=s4.at[k, e], recv_sem=r4.at[k],
            device_id={"pb": lax.rem(b + e, B)}, device_id_type=MESH,
        )

    def give_half(k, h):
        for e in range(1, B):
            @pl.when(lax.rem(b + e, B) == h)
            def _():
                to_half(k, h, e).start()

    def sum_half(k):
        for e in range(1, B):
            to_half(k, b, e).wait_recv()
        for e in list(range(1, R)) + [0]:
            row = lax.rem(r + e, R)
            for s in range(share):
                value = part[k, b, row, s].astype(f32)
                for p in range(B - 1):
                    value = value + got1[k, p, row, s].astype(f32)
                half[k, e, s] = value.astype(bf16)
            if e:
                to_row(k, e).start()

    def sum_row(k):
        for e in range(1, R):
            to_row(k, e).wait_recv()
        for s in range(share):
            value = half[k, 0, s].astype(f32)
            for e in range(1, R):
                value = value + got2[k, e, s].astype(f32)
            block[k, s] = value.astype(bf16)

            @pl.when(b * share + s != c)
            def _():
                to_col(k, s, c).start()

    mine = near == b

    def sum_col(k):
        @pl.when(mine)
        def _():
            value = block[k, c - b * share].astype(f32)
            for e in range(1, C):
                src = lax.rem(c + e, C)
                to_col(k, 0, src).wait_recv()
                value = value + got3[k, src].astype(f32)
            final[k] = value
            for e in range(1, B):
                to_pb(k, e).start()

    weight = None
    wait_all((B_FIRST,))
    for k in (0, 2):
        def prime_b(h, carry):
            prime(1, k, h)
            return carry

        def dress_b(h, carry):
            dress(1, k, h, weight)
            give_half(k, h)
            return carry

        lax.fori_loop(0, B, prime_b, 0)
        if weight is None:
            weight = occupied(1)
        lax.fori_loop(0, B, dress_b, 0)
    sum_half(0)
    sum_half(2)

    def last(t, carry):
        h = lax.rem(near + t, B)

        @pl.when(t == 1)
        def _():
            sum_row(0)
            sum_row(2)

            @pl.when(mine)
            def _():
                sum_half(1)

        def one(q, inner):
            wait_from((B_LAST,), lax.div(q, share) * C + h * share + lax.rem(q, share))
            return inner

        lax.fori_loop(0, R * share, one, 0)
        prime(1, 1, h)
        dress(1, 1, h, weight)
        give_half(1, h)
        return carry

    lax.fori_loop(0, B, last, 0)

    @pl.when(jnp.logical_not(mine))
    def _():
        sum_half(1)

    sum_col(0)
    sum_col(2)
    for i in range(C):
        put_out(0, i).wait()
    unpermute(1)
    sum_row(1)
    sum_col(1)

    @pl.when(jnp.logical_not(mine))
    def _():
        for k in range(3):
            to_pb(k, 1).wait_recv()

    value = jnp.zeros((rw, cw), f32)
    for k in range(3):
        hi = final[k].astype(bf16)
        lo = (final[k] - hi.astype(f32)).astype(bf16)
        value = value + dot(hi, back[k * LANE : (k + 1) * LANE]) + dot(lo, back[k * LANE : (k + 1) * LANE])
    fock[...] = value

    def drain(m, carry):
        for kind in range(5):
            move(kind, m, me).wait_send()
        return carry

    lax.fori_loop(0, N - 1, drain, 0)
    for to in others:
        amp_move(to, r).wait_send()
    for k in range(3):
        for e in range(1, B):
            to_half(k, b, e).wait_send()
        for e in range(1, R):
            to_row(k, e).wait_send()
        for s in range(share):
            @pl.when(b * share + s != c)
            def _():
                to_col(k, s, c).wait_send()

        @pl.when(mine)
        def _():
            for e in range(1, B):
                to_pb(k, e).wait_send()
    for i in range(C):
        put_out(1, i).wait()


def finish_kernel(before, fock_in, dressed, fock, held, sem):
    pieces = held.shape[0]
    step = dressed.shape[1] // (pieces // 2)
    where = [(v, pl.ds(k * step, step)) for v in range(2) for k in range(pieces // 2)]
    loads = [pltpu.make_async_copy(before.at[w], held.at[p], sem.at[0, p]) for p, w in enumerate(where)]
    stores = [pltpu.make_async_copy(held.at[p], dressed.at[w], sem.at[1, p]) for p, w in enumerate(where)]
    for copy in loads:
        copy.start()
    fock[...] = fock_in[...]
    for copy, out in zip(loads, stores):
        copy.wait()
        out.start()
    for out in stores:
        out.wait()


def local(chol, amplitudes):
    B, R, C = lax.axis_size("pb"), lax.axis_size("row"), lax.axis_size("col")
    q_local, rw, cw = chol.shape
    n = cw // rw
    norb = C * cw
    occ = amplitudes.shape[0]
    groups = rw // SH
    mid = 64
    low = cw - 2 * LANE - mid
    rows = 2 * rw // 7
    share = C // B
    N = R * C
    virtual = np.arange(groups * VG)
    widen = virtual[:, None] // VG * SH + OG + virtual[:, None] % VG == np.arange(rw)[None, :]
    index = np.arange(occ)
    place = np.arange(norb)[:, None] == (index // OG * SH + index % OG)[None, :]
    place = place.reshape(C, cw, occ)
    column = np.arange(cw)
    order = np.concatenate([column[column % SH < OG], column[column % SH >= OG]])
    perm = np.zeros((cw, 3 * LANE), bool)
    perm[order, np.arange(cw)] = True
    per_block = occ // C
    occ_of = np.zeros((C, LANE, occ), bool)
    for j in range(C):
        occ_of[j, np.arange(per_block), j * per_block + np.arange(per_block)] = True
    occ_of = occ_of.reshape(B, share * LANE, occ)
    const = lambda array: jnp.asarray(array, bf16)
    hbm = pl.BlockSpec(memory_space=pl.ANY)
    vmem = pl.BlockSpec(memory_space=pltpu.VMEM)
    dma = pltpu.SemaphoreType.DMA
    half_width = lambda *shape: pltpu.VMEM(shape, bf16)
    full_width = lambda *shape: pltpu.VMEM(shape, f32)
    before, fock_in = pl.pallas_call(
        functools.partial(main_kernel, B, R, C, n, mid, low, rows),
        out_shape=(
            jax.ShapeDtypeStruct((2, norb, norb), bf16),
            jax.ShapeDtypeStruct((rw, cw), f32),
        ),
        in_specs=[hbm] + [vmem] * 7,
        out_specs=(hbm, vmem),
        scratch_shapes=[
            half_width(SLOTS, 2, rw, cw),
            half_width(N, 2, 2, rw, LANE),
            half_width(N, rw, LANE),
            half_width(N, rows, LANE),
            half_width(N, rw, LANE),
            half_width(N, rows, LANE),
            half_width(2, 3, C, R, rw, LANE),
            half_width(2, 3, C, C, cw, LANE),
            full_width(3, C, C, cw, LANE),
            half_width(occ, rw),
            half_width(R, occ, rw),
            half_width(C, occ, cw),
            half_width(3, C, occ, LANE),
            half_width(2, C, cw, occ),
            half_width(3, B, R, share, rw, LANE),
            half_width(3, B - 1, R, share, rw, LANE),
            half_width(3, R, share, rw, LANE),
            half_width(3, R, share, rw, LANE),
            half_width(3, share, rw, LANE),
            half_width(3, C, rw, LANE),
            full_width(3, rw, LANE),
            half_width(C, cw, norb),
            dma((5, N)), dma((5, N)), dma((R,)), dma((R,)), dma((SLOTS,)),
            dma((3, B)), dma((3, B)), dma((3, R)), dma((3, R)), dma((3, share)), dma((3, C)), dma((3, B)), dma((3,)),
            dma((C,)),
        ],
        compiler_params=pltpu.CompilerParams(
            collective_id=0, has_side_effects=True, vmem_limit_bytes=63 * 1024 * 1024
        ),
        name="exchange",
    )(chol, amplitudes, const(widen), const(perm), const(perm.T), const(place),
      const(place.transpose(0, 2, 1)), const(occ_of))
    return pl.pallas_call(
        finish_kernel,
        out_shape=(
            jax.ShapeDtypeStruct((2, norb, norb), bf16),
            jax.ShapeDtypeStruct((rw, cw), f32),
        ),
        in_specs=[hbm, vmem],
        out_specs=(hbm, vmem),
        scratch_shapes=[half_width(2 * C, cw, norb), dma((2, 2 * C))],
        compiler_params=pltpu.CompilerParams(vmem_limit_bytes=16 * 1024 * 1024),
        name="finish",
    )(before, fock_in)


def solution(mesh):
    return jax.shard_map(
        local,
        mesh=mesh,
        in_specs=(P("pb", "row", "col"), P(None, "row")),
        out_specs=(P(("pb", "row", "col"), None, None), P("row", "col")),
        check_vma=False,
    )
```

time: 232 us -> 237 us (1.022); the launches traced: 228 us -> 237 us
  Pallas kernels: 225 us -> 232 us
    pallas_call x3 -> x2, Pallas kernels: 225 us -> 232 us  [the longest x1 226 us: local(): pl.pallas_call(functools.partial(main_kernel, B, R, C, n, mid, low, rows)...]
where the time goes in v1:
time: 237 us
  Pallas kernels  232 us (98%)
  local copies, waits for them, and re-layouts  4.18 us (2%)
    pallas_call x1, Pallas kernels, local(): pl.pallas_call(functools.partial(main_kernel, B, R, C, n, mid, low, rows)...  226 us
    pallas_call x1, Pallas kernels, local(): pl.pallas_call(finish_kernel, out_shape=(jax.ShapeDtypeStruct((2, norb, n...  6.08 us

profile of v1, /device:TPU:1, one launch (start us, length us, event | category | flops | bytes accessed | tf_op | source)
XLA Modules:
  0.0 236.7 jit_solution(13159310475893392457)
XLA Ops:
  0.6 225.8 %exchange.1 = (bf16[2,1344,1344]{2,1,0:T(8,128)(2,1)}, f32[336,336]{1,0:T(8,128)}) custom-call(bf16[32,336,336]{2,1,0:T(8,128)(2,1)} %chol.1, bf16[144,300]{1,0:T(8,128)(2,1)} %amp.1, bf16[300,336]{1,0:T(8,128)(2,1)} %constant.12.clone.widen, bf16[336,384]{1,0:T(8,128)(2,1)} %constant.13.clone.perm, bf16[384,336]{1,0:T(8,128)(2,1)} %constant.14.clone.back, ...), custom_call_target="tpu_custom_call" | custom-call | tf_op jit(solution)/shard_map/exchange/pallas_call | solution.py:496
  226.4 0.0 copy-start
  226.4 3.1 %copy-done = bf16[2,1344,1344]{2,1,0:T(8,128)(2,1)S(1)} copy-done((bf16[2,1344,1344]{2,1,0:T(8,128)(2,1)S(1)}, bf16[2,1344,1344]{2,1,0:T(8,128)(2,1)}, u32[]{:S(2)}) %copy-start) | copy-done | bytes 7225368
  229.6 0.0 copy-start.1
  229.6 1.0 copy-done.1
  230.6 6.1 %finish.1 = (bf16[2,1344,1344]{2,1,0:T(8,128)(2,1)}, f32[336,336]{1,0:T(8,128)}) custom-call(bf16[2,1344,1344]{2,1,0:T(8,128)(2,1)S(1)} %copy-done, f32[336,336]{1,0:T(8,128)S(1)} %copy-done.1), custom_call_target="tpu_custom_call" | custom-call | tf_op jit(solution)/shard_map/finish/pallas_call | solution.py:537
Async XLA Ops:
  226.4 3.1 %copy-start = (bf16[2,1344,1344]{2,1,0:T(8,128)(2,1)S(1)}, bf16[2,1344,1344]{2,1,0:T(8,128)(2,1)}, u32[]{:S(2)}) copy-start(bf16[2,1344,1344]{2,1,0:T(8,128)(2,1)} %get-tuple-element.4.before) | copy-start | bytes 21676036
  229.6 1.0 copy-start.1

commit v2 on v1

--- a/solution.py
+++ b/solution.py
@@ -51,16 +51,18 @@
 
 
 SLOTS = 4
-A_MAIN, WIDE, THIN, B_FIRST, B_LAST = range(5)
+MAIN_VMEM = 54 * 1024 * 1024
+FIRST, WIDE, THIN, A_LAST, B_LAST = range(5)
 
 
 def main_kernel(
-    B, R, C, n, mid, low, rows, chol, amp, widen, perm, back, pick, pick_t, occ_of,
+    B, R, C, n, mid, low, rows, chol, amp_in, perm_in, widen_in, back_in, pick_in, pick_t_in, occ_of_in,
     dressed, fock,
-    stage, packed, wide_out, thin_out, wides, thins, x, d, total, amp_out, amp_all, amps, amp_perm, cols,
-    part, got1, half, got2, block, got3, final, strips,
-    send, recv, amp_send, amp_recv, load, s1, r1, s2, r2, s3, r3, s4, r4, out_sem,
+    stage, packed, wide_out, thin_out, wides, thins, x, total, amp_out, amp_all, amps, amp_perm, cols,
+    part, got1, half, got2, block, got3, final, perm, amp, widen, back, pick, pick_t, occ_of,
+    send, recv, amp_send, amp_recv, load, table, s1, r1, s2, r2, s3, r3, s4, r4, *taller,
 ):
+    d = taller[0] if taller else x
     b, r, c = lax.axis_index("pb"), lax.axis_index("row"), lax.axis_index("col")
     me = r * C + c
     N = R * C
@@ -79,27 +81,29 @@
         slot = lax.rem(m, SLOTS)
         return pltpu.make_async_copy(chol.at[pl.ds((row * C + col) * 2, 2)], stage.at[slot], load.at[slot])
 
-    for m in range(SLOTS):
-        fetch(m).start()
     barrier = pltpu.get_barrier_semaphore()
     for m in range(N - 1):
         row, col = place(m)
         pl.semaphore_signal(barrier, inc=1, device_id={"row": row, "col": col}, device_id_type=MESH)
     for e in range(1, B):
         pl.semaphore_signal(barrier, inc=1, device_id={"pb": lax.rem(b + e, B)}, device_id_type=MESH)
-    own_amp = dot(amp[...], widen[...]).astype(bf16)
-    amp_out[...] = own_amp
-    amp_all[r] = own_amp
+    tables = [(perm_in, perm), (amp_in, amp), (widen_in, widen), (back_in, back),
+              (pick_in, pick), (pick_t_in, pick_t), (occ_of_in, occ_of)]
+    tables = [pltpu.make_async_copy(src, dst, table.at[i]) for i, (src, dst) in enumerate(tables)]
+    tables[0].start()
+    for m in range(SLOTS):
+        fetch(m).start()
+    tables[0].wait()
     pl.semaphore_wait(barrier, N - 1 + B - 1)
 
     def move(kind, m, src_rank):
         row, col = place(m)
         from_row, from_col = lax.div(src_rank, C), lax.rem(src_rank, C)
         src, dst = {
-            A_MAIN: (packed.at[m, 0], x.at[0, pl.ds(0, 2), from_col, from_row]),
+            FIRST: (packed.at[m, pl.ds(0, 2), 0], x.at[pl.ds(0, 2), 0, from_col, from_row]),
             WIDE: (wide_out.at[m], wides.at[src_rank]),
             THIN: (thin_out.at[m], thins.at[src_rank]),
-            B_FIRST: (packed.at[m, 1, 0], x.at[1, 0, from_col, from_row]),
+            A_LAST: (packed.at[m, 0, 1], x.at[0, 1, from_col, from_row]),
             B_LAST: (packed.at[m, 1, 1], x.at[1, 1, from_col, from_row]),
         }[kind]
         return pltpu.make_async_remote_copy(
@@ -119,7 +123,7 @@
 
         @pl.when(m < N - 1)
         def _():
-            move(A_MAIN, m, me).start()
+            move(FIRST, m, me).start()
 
         wide, thin = pack(tails[0], tails[1], mid, low, rows)
         wide_out[m] = wide
@@ -132,6 +136,13 @@
         return carry
 
     lax.fori_loop(0, N, permute, 0)
+    for copy in tables[1:]:
+        copy.start()
+    for copy in tables[1:]:
+        copy.wait()
+    own_amp = dot(amp[...], widen[...]).astype(bf16)
+    amp_out[...] = own_amp
+    amp_all[r] = own_amp
 
     def amp_move(to, src):
         return pltpu.make_async_remote_copy(
@@ -151,9 +162,18 @@
 
         lax.fori_loop(0, N - 1, one, 0)
 
-    start_all((WIDE, THIN))
-    start_all((B_FIRST,))
-    start_all((B_LAST,))
+    inner = (c > 0) & (c < C - 1)
+
+    @pl.when(inner)
+    def _():
+        for kinds in ((WIDE, THIN), (A_LAST,), (B_LAST,)):
+            start_all(kinds)
+
+    def release(kinds):
+        @pl.when(jnp.logical_not(inner))
+        def _():
+            start_all(kinds)
+
     for v in range(2):
         for k in range(2):
             x[v, k, c, r] = packed[N - 1, v, k]
@@ -233,17 +253,14 @@
             for s in range(share):
                 mine = value[:, s * LANE : (s + 1) * LANE]
                 if v == 0:
-                    total[k, h * share + s, i] = mine
+                    total[h * share + s, i] = mine
                 else:
-                    mine = total[k, h * share + s, i] + mine
+                    mine = total[h * share + s, i] + mine
                     for m in range(n):
                         part[k, h, i * n + m, s] = mine[m * rw : (m + 1) * rw].astype(bf16)
             return carry
 
         lax.fori_loop(0, C, put, 0)
-
-    def put_out(v, i):
-        return pltpu.make_async_copy(strips.at[i], dressed.at[v, pl.ds(i * th, th), :], out_sem.at[i])
 
     def unpermute(v):
         def one(i, carry):
@@ -251,36 +268,10 @@
             for j in range(C):
                 ordered = jnp.concatenate([d[v, k, j, i] for k in range(3)], axis=1)
                 natural.append(dot(ordered, back[...]))
-            strips[i] = jnp.concatenate(natural, axis=1).astype(bf16)
-            put_out(v, i).start()
+            dressed[v, pl.ds(pl.multiple_of(i * th, 8), th), :] = jnp.concatenate(natural, axis=1).astype(bf16)
             return carry
 
         lax.fori_loop(0, C, one, 0)
-
-    wait_all((A_MAIN,))
-    wait_all((WIDE, THIN))
-
-    def open_tail(s, carry):
-        row, col = lax.div(s, C), lax.rem(s, C)
-        for v, value in enumerate(unpack(wides[s], thins[s], mid, low, rw)):
-            x[v, 2, col, row] = value
-        return carry
-
-    lax.fori_loop(0, N, open_tail, 0)
-
-    def prime_a(t, carry):
-        prime(0, lax.div(t, B), lax.rem(t, B))
-        return carry
-
-    lax.fori_loop(0, 3 * B, prime_a, 0)
-    weight_a = occupied(0)
-
-    def dress_a(t, carry):
-        dress(0, lax.div(t, B), lax.rem(t, B), weight_a)
-        return carry
-
-    lax.fori_loop(0, 3 * B, dress_a, 0)
-    unpermute(0)
 
     def to_half(k, h, e):
         return pltpu.make_async_remote_copy(
@@ -352,33 +343,53 @@
             for e in range(1, B):
                 to_pb(k, e).start()
 
-    weight = None
-    wait_all((B_FIRST,))
-    for k in (0, 2):
-        def prime_b(h, carry):
-            prime(1, k, h)
-            return carry
-
-        def dress_b(h, carry):
-            dress(1, k, h, weight)
-            give_half(k, h)
-            return carry
-
-        lax.fori_loop(0, B, prime_b, 0)
-        if weight is None:
-            weight = occupied(1)
-        lax.fori_loop(0, B, dress_b, 0)
+    def open_tail(s, carry):
+        row, col = lax.div(s, C), lax.rem(s, C)
+        for v, value in enumerate(unpack(wides[s], thins[s], mid, low, rw)):
+            x[v, 2, col, row] = value
+        return carry
+
+    def primes(k, first, last):
+        def one(t, carry):
+            prime(lax.div(t, B), k, lax.rem(t, B))
+            return carry
+
+        lax.fori_loop(first * B, last * B, one, 0)
+
+    def dresses(v, k):
+        def one(h, carry):
+            dress(v, k, h, weight[v])
+            if v:
+                give_half(k, h)
+            return carry
+
+        lax.fori_loop(0, B, one, 0)
+
+    wait_all((FIRST,))
+    release((WIDE, THIN))
+    primes(0, 0, 2)
+    weight = [occupied(v) for v in range(2)]
+    dresses(0, 0)
+    dresses(1, 0)
     sum_half(0)
+    wait_all((WIDE, THIN))
+    release((A_LAST,))
+    lax.fori_loop(0, N, open_tail, 0)
+    primes(2, 0, 2)
+    dresses(0, 2)
+    dresses(1, 2)
     sum_half(2)
+    wait_all((A_LAST,))
+    release((B_LAST,))
+    primes(1, 0, 1)
+    dresses(0, 1)
+    unpermute(0)
 
     def last(t, carry):
         h = lax.rem(near + t, B)
 
         @pl.when(t == 1)
         def _():
-            sum_row(0)
-            sum_row(2)
-
             @pl.when(mine)
             def _():
                 sum_half(1)
@@ -388,8 +399,14 @@
             return inner
 
         lax.fori_loop(0, R * share, one, 0)
+
+        @pl.when(t == B - 1)
+        def _():
+            sum_row(0)
+            sum_row(2)
+
         prime(1, 1, h)
-        dress(1, 1, h, weight)
+        dress(1, 1, h, weight[1])
         give_half(1, h)
         return carry
 
@@ -401,8 +418,6 @@
 
     sum_col(0)
     sum_col(2)
-    for i in range(C):
-        put_out(0, i).wait()
     unpermute(1)
     sum_row(1)
     sum_col(1)
@@ -441,24 +456,13 @@
         def _():
             for e in range(1, B):
                 to_pb(k, e).wait_send()
-    for i in range(C):
-        put_out(1, i).wait()
-
-
-def finish_kernel(before, fock_in, dressed, fock, held, sem):
-    pieces = held.shape[0]
-    step = dressed.shape[1] // (pieces // 2)
-    where = [(v, pl.ds(k * step, step)) for v in range(2) for k in range(pieces // 2)]
-    loads = [pltpu.make_async_copy(before.at[w], held.at[p], sem.at[0, p]) for p, w in enumerate(where)]
-    stores = [pltpu.make_async_copy(held.at[p], dressed.at[w], sem.at[1, p]) for p, w in enumerate(where)]
-    for copy in loads:
-        copy.start()
+
+
+def finish_kernel(before, fock_in, dressed, fock, sem):
+    store = pltpu.make_async_copy(before, dressed, sem)
+    store.start()
     fock[...] = fock_in[...]
-    for copy, out in zip(loads, stores):
-        copy.wait()
-        out.start()
-    for out in stores:
-        out.wait()
+    store.wait()
 
 
 def local(chol, amplitudes):
@@ -493,14 +497,14 @@
     dma = pltpu.SemaphoreType.DMA
     half_width = lambda *shape: pltpu.VMEM(shape, bf16)
     full_width = lambda *shape: pltpu.VMEM(shape, f32)
+    tables = [perm, widen, perm.T, place, place.transpose(0, 2, 1), occ_of]
+    tables = [const(array) for array in tables]
+    room = lambda array: half_width(*array.shape)
     before, fock_in = pl.pallas_call(
         functools.partial(main_kernel, B, R, C, n, mid, low, rows),
-        out_shape=(
-            jax.ShapeDtypeStruct((2, norb, norb), bf16),
-            jax.ShapeDtypeStruct((rw, cw), f32),
-        ),
-        in_specs=[hbm] + [vmem] * 7,
-        out_specs=(hbm, vmem),
+        out_shape=(pltpu.VMEM((2, norb, norb), bf16), pltpu.VMEM((rw, cw), f32)),
+        in_specs=[hbm] * (2 + len(tables)),
+        out_specs=(vmem, vmem),
         scratch_shapes=[
             half_width(SLOTS, 2, rw, cw),
             half_width(N, 2, 2, rw, LANE),
@@ -509,8 +513,7 @@
             half_width(N, rw, LANE),
             half_width(N, rows, LANE),
             half_width(2, 3, C, R, rw, LANE),
-            half_width(2, 3, C, C, cw, LANE),
-            full_width(3, C, C, cw, LANE),
+            full_width(C, C, cw, LANE),
             half_width(occ, rw),
             half_width(R, occ, rw),
             half_width(C, occ, cw),
@@ -523,26 +526,27 @@
             half_width(3, share, rw, LANE),
             half_width(3, C, rw, LANE),
             full_width(3, rw, LANE),
-            half_width(C, cw, norb),
-            dma((5, N)), dma((5, N)), dma((R,)), dma((R,)), dma((SLOTS,)),
+            room(tables[0]),
+            room(amplitudes),
+            *[room(array) for array in tables[1:]],
+            dma((5, N)), dma((5, N)), dma((R,)), dma((R,)), dma((SLOTS,)), dma((1 + len(tables),)),
             dma((3, B)), dma((3, B)), dma((3, R)), dma((3, R)), dma((3, share)), dma((3, C)), dma((3, B)), dma((3,)),
-            dma((C,)),
+            *([half_width(2, 3, C, C, cw, LANE)] if n > 1 else []),
         ],
         compiler_params=pltpu.CompilerParams(
-            collective_id=0, has_side_effects=True, vmem_limit_bytes=63 * 1024 * 1024
+            collective_id=0, has_side_effects=True, vmem_limit_bytes=MAIN_VMEM
         ),
         name="exchange",
-    )(chol, amplitudes, const(widen), const(perm), const(perm.T), const(place),
-      const(place.transpose(0, 2, 1)), const(occ_of))
+    )(chol, amplitudes, *tables)
     return pl.pallas_call(
         finish_kernel,
         out_shape=(
             jax.ShapeDtypeStruct((2, norb, norb), bf16),
             jax.ShapeDtypeStruct((rw, cw), f32),
         ),
-        in_specs=[hbm, vmem],
+        in_specs=[vmem, vmem],
         out_specs=(hbm, vmem),
-        scratch_shapes=[half_width(2 * C, cw, norb), dma((2, 2 * C))],
+        scratch_shapes=[dma(())],
         compiler_params=pltpu.CompilerParams(vmem_limit_bytes=16 * 1024 * 1024),
         name="finish",
     )(before, fock_in)

time: 237 us -> 191 us (0.81)
  Pallas kernels: 232 us -> 191 us
  local copies, waits for them, and re-layouts: 4.18 us -> 0 us
    pallas_call x1, Pallas kernels: 226 us -> 187 us  [local(): pl.pallas_call(functools.partial(main_kernel, B, R, C, n, mid, low, rows)...]
    unnamed x4 -> x0, local copies, waits for them, and re-layouts: 4.18 us -> none
where the time goes in v2:
time: 191 us
  Pallas kernels  191 us (100%)
    pallas_call x1, Pallas kernels, local(): pl.pallas_call(functools.partial(main_kernel, B, R, C, n, mid, low, rows)...  187 us
    pallas_call x1, Pallas kernels, local(): pl.pallas_call(finish_kernel, out_shape=(jax.ShapeDtypeStruct((2, norb, n...  3.92 us

profile of v2, /device:TPU:1, one launch (start us, length us, event | category | flops | bytes accessed | tf_op | source)
XLA Modules:
  0.0 191.2 jit_solution(17295930603784841088)
XLA Ops:
  0.6 186.7 %exchange.1 = (bf16[2,1344,1344]{2,1,0:T(8,128)(2,1)S(1)}, f32[336,336]{1,0:T(8,128)S(1)}) custom-call(bf16[32,336,336]{2,1,0:T(8,128)(2,1)} %chol.1, bf16[144,300]{1,0:T(8,128)(2,1)} %amp_in.1, bf16[336,384]{1,0:T(8,128)(2,1)} %constant.12.clone.perm_in, bf16[300,336]{1,0:T(8,128)(2,1)} %constant.13.clone.widen_in, ...), custom_call_target="tpu_custom_call" | custom-call | tf_op jit(solution)/shard_map/exchange/pallas_call | solution.py:503
  187.3 3.9 %finish.1 = (bf16[2,1344,1344]{2,1,0:T(8,128)(2,1)}, f32[336,336]{1,0:T(8,128)}) custom-call(bf16[2,1344,1344]{2,1,0:T(8,128)(2,1)S(1)} %get-tuple-element.4.before, f32[336,336]{1,0:T(8,128)S(1)} %get-tuple-element.5.fock_in), custom_call_target="tpu_custom_call" | custom-call | tf_op jit(solution)/shard_map/finish/pallas_call | solution.py:541

commit v3 on v2

v3 whole, which is shorter than its diff:
```python
import functools
import jax
import numpy as np
import jax.numpy as jnp
from jax import lax
from jax.experimental import pallas as pl
from jax.experimental.pallas import tpu as pltpu
from jax.sharding import PartitionSpec as P

OG = 9
VG = 75
SH = 84
LANE = 128
MESH = pl.DeviceIdType.MESH
f32, bf16 = jnp.float32, jnp.bfloat16


def dot(a, b):
    return jnp.dot(a, b, preferred_element_type=f32)


def peer(index, mode, size):
    if size & (size - 1):
        return lax.rem(index + mode, size)
    bits = [1 << k for k in range(size.bit_length() - 1)]
    flip = lambda bit: lax.rem(lax.rem(lax.div(index, bit), 2) + lax.rem(lax.div(mode, bit), 2), 2) * bit
    return sum(flip(bit) for bit in bits)


def lanes(parts):
    return jnp.concatenate([p.astype(f32) for p in parts], axis=1).astype(bf16)


def pack(first, second, mid, low, rows):
    wide = jnp.concatenate([first[:, :mid], second[:, :mid]], axis=1).astype(bf16)
    thin = jnp.concatenate([first[:, mid:], second[:, mid:]], axis=0)
    pieces = [thin[k * rows : (k + 1) * rows] for k in range(thin.shape[0] // rows)]
    pieces.append(jnp.zeros((rows, LANE - low * len(pieces)), f32))
    return wide, jnp.concatenate(pieces, axis=1).astype(bf16)


def unpack(wide, thin, mid, low, rw):
    wide, thin = wide.astype(f32), thin.astype(f32)
    rows = thin.shape[0]
    pieces = [thin[:, k * low : (k + 1) * low] for k in range(2 * rw // rows)]
    thin = jnp.concatenate(pieces, axis=0)
    blank = jnp.zeros((rw, LANE - mid - low), f32)
    for v in range(2):
        part = [wide[:, v * mid : (v + 1) * mid], thin[v * rw : (v + 1) * rw], blank]
        yield jnp.concatenate(part, axis=1).astype(bf16)


SLOTS = 4
MAIN_VMEM = 54 * 1024 * 1024
FIRST, WIDE, THIN, A_LAST, B_LAST = range(5)
NEAR, PAIR, FAR = range(3)
EARLY = (0, 2)


def main_kernel(
    B, R, C, n, mid, low, rows, chol, amp_in, perm_in, widen_in, back_in, pick_in, pick_t_in, occ_of_in,
    dressed, fock,
    stage, packed, wide_out, thin_out, wides, thins, x, total, amp_out, amp_all, joint, amp_perm, cols, square, free,
    part, got1, half, got2, block, got3, final, perm, amp, widen, back, pick, pick_t, occ_of,
    send, recv, recv_last, amp_sem, load, table, s1, r1, s2, r2, s3, r3, s4, r4, *taller,
):
    d = taller[0] if taller else x
    b, r, c = lax.axis_index("pb"), lax.axis_index("row"), lax.axis_index("col")
    me = r * C + c
    N = R * C
    share = C // B
    rw, cw = chol.shape[1], chol.shape[2]
    th = rw * n
    near = lax.div(c, share)

    def place(m):
        k = lax.rem(lax.div(m, 2) + lax.rem(m, 2), N // 2)
        dc = lax.rem(k, C // 2) + (C // 2) * (1 - lax.rem(m, 2))
        return peer(r, lax.div(k, C // 2), R), peer(c, dc, C)

    def fetch(m):
        row, col = place(m)
        slot = lax.rem(m, SLOTS)
        return pltpu.make_async_copy(chol.at[pl.ds((row * C + col) * 2, 2)], stage.at[slot], load.at[slot])

    barrier = pltpu.get_barrier_semaphore()
    for m in range(N - 1):
        row, col = place(m)
        pl.semaphore_signal(barrier, inc=1, device_id={"row": row, "col": col}, device_id_type=MESH)
    for e in range(1, B):
        pl.semaphore_signal(barrier, inc=1, device_id={"pb": lax.rem(b + e, B)}, device_id_type=MESH)
    tables = [(perm_in, perm), (amp_in, amp), (widen_in, widen), (back_in, back),
              (pick_in, pick), (pick_t_in, pick_t), (occ_of_in, occ_of)]
    tables = [pltpu.make_async_copy(src, dst, table.at[i]) for i, (src, dst) in enumerate(tables)]
    tables[0].start()
    for m in range(SLOTS):
        fetch(m).start()
    tables[0].wait()

    def bytes_of(ref, sem):
        return pltpu.make_async_copy(ref, ref, sem)

    others = pl.ds(0, N - 1)
    every = {
        FIRST: packed.at[others, pl.ds(0, 2), 0],
        WIDE: wide_out.at[others],
        THIN: thin_out.at[others],
        A_LAST: packed.at[others, 0, 1],
        B_LAST: packed.at[others, 1, 1],
    }

    def move(kind, m):
        row, col = place(m)
        src, dst = {
            FIRST: (packed.at[m, pl.ds(0, 2), 0], x.at[pl.ds(0, 2), 0, c, r]),
            WIDE: (wide_out.at[m], wides.at[me]),
            THIN: (thin_out.at[m], thins.at[me]),
            A_LAST: (packed.at[m, 0, 1], x.at[0, 1, c, r]),
            B_LAST: (packed.at[m, 1, 1], x.at[1, 1, c, r]),
        }[kind]
        turn = lax.rem(near - lax.div(col, share) + B, B)
        return pltpu.make_async_remote_copy(
            src_ref=src, dst_ref=dst, send_sem=send.at[kind],
            recv_sem=recv_last.at[turn] if kind == B_LAST else recv.at[kind],
            device_id={"row": row, "col": col}, device_id_type=MESH,
        )

    def wait_all(kinds):
        for kind in kinds:
            bytes_of(every[kind], recv.at[kind]).wait()

    def wait_last(turn):
        count = R * share - (turn == 0)
        bytes_of(packed.at[pl.ds(0, count), 1, 1], recv_last.at[turn]).wait()

    def order_columns(m):
        fetch(m).wait()
        slot = lax.rem(m, SLOTS)
        tails = []
        for v in range(2):
            y = dot(stage[slot, v], perm[...])
            packed[m, v, 0] = y[:, :LANE].astype(bf16)
            packed[m, v, 1] = y[:, LANE : 2 * LANE].astype(bf16)
            tails.append(y[:, 2 * LANE : 2 * LANE + mid + low])
        return tails

    def pack_tails(m, tails):
        wide, thin = pack(tails[0], tails[1], mid, low, rows)
        wide_out[m] = wide
        thin_out[m] = thin

        @pl.when(m + SLOTS < N)
        def _():
            fetch(m + SLOTS).start()

    def permute(m, carry):
        tails = order_columns(m)

        @pl.when(m < N - 1)
        def _():
            move(FIRST, m).start()

        pack_tails(m, tails)
        return carry

    first_tails = order_columns(0)
    pl.semaphore_wait(barrier, N - 1 + B - 1)
    move(FIRST, 0).start()
    pack_tails(0, first_tails)
    lax.fori_loop(1, N, permute, 0)
    for copy in tables[1:]:
        copy.start()
    for copy in tables[1:]:
        copy.wait()
    own_amp = dot(amp[...], widen[...]).astype(bf16)
    amp_out[...] = own_amp
    amp_all[r] = own_amp

    def amp_move(k):
        return pltpu.make_async_remote_copy(
            src_ref=amp_out, dst_ref=amp_all.at[r], send_sem=amp_sem.at[0], recv_sem=amp_sem.at[1],
            device_id={"row": peer(r, k, R)}, device_id_type=MESH,
        )

    for k in range(1, R):
        amp_move(k).start()

    def start_all(kinds):
        def one(m, carry):
            for kind in kinds:
                move(kind, m).start()
            return carry

        lax.fori_loop(0, N - 1, one, 0)

    inner = (c > 0) & (c < C - 1)

    @pl.when(inner)
    def _():
        for kinds in ((WIDE, THIN), (A_LAST,), (B_LAST,)):
            start_all(kinds)

    def release(kinds):
        @pl.when(jnp.logical_not(inner))
        def _():
            start_all(kinds)

    for v in range(2):
        for k in range(2):
            x[v, k, c, r] = packed[N - 1, v, k]
    wides[me] = wide_out[N - 1]
    thins[me] = thin_out[N - 1]
    ones = jnp.ones((pick.shape[2], share * LANE), bf16)
    free[...] = 1.0 - dot(pick[0], ones)
    bytes_of(amp_all.at[pl.ds(0, R - 1)], amp_sem.at[1]).wait()
    for i in range(C):
        whole = amp_all[i] if n == 1 else lanes([amp_all[i * n + m] for m in range(n)])
        joint[i] = (pick_t[i].astype(f32) - whole.astype(f32)).astype(bf16)
        ordered = dot(whole, perm[...]).astype(bf16)
        for k in range(3):
            amp_perm[k, i] = ordered[:, k * LANE : (k + 1) * LANE]

    def side(ref, h):
        return jnp.concatenate([ref[h * share + s] for s in range(share)], axis=1)

    def arrived(v, k, h, i):
        if n == 1:
            return side(x.at[v, k, :, i], h)
        tall = [side(x.at[v, k, :, i * n + m], h).astype(f32) for m in range(n)]
        return jnp.concatenate(tall, axis=0).astype(bf16)

    def loop(body, start, fast):
        if not fast:
            return lax.fori_loop(0, C, body, start)
        for i in range(C):
            start = body(i, start)
        return start

    def occ_rows(v, k, h, start, fast=False):
        return loop(lambda i, rows: rows + dot(joint[i], arrived(v, k, h, i)), start, fast)

    def occupied(v):
        blank = jnp.zeros((joint.shape[1], share * LANE), f32)
        block_of = sum(dot(occ_rows(v, 0, h, blank).astype(bf16), occ_of[h]) for h in range(B))
        square[v] = block_of.astype(bf16)
        corner = block_of.astype(bf16)

        def one(i, carry):
            virtual = sum(dot(arrived(v, 0, h, i), occ_of[h]) for h in range(B)) * free[:, : virtual_width]
            cols[v, i] = (virtual + dot(pick[i], corner)).astype(bf16)
            return carry

        virtual_width = corner.shape[1]
        lax.fori_loop(0, C, one, 0)
        shape = block_of.shape
        on = lax.broadcasted_iota(jnp.int32, shape, 0) == lax.broadcasted_iota(jnp.int32, shape, 1)
        diag = jnp.where(on, corner.astype(f32), 0.0)
        return jnp.sum(jnp.sum(diag, axis=1, keepdims=True), axis=0, keepdims=True)

    def to_half(k, h, e, i):
        to, of = lax.rem(b + e, B), pl.ds(i * n, n)
        return pltpu.make_async_remote_copy(
            src_ref=part.at[k, h, to, of], dst_ref=got1.at[k, h, e - 1, of], send_sem=s1.at[k, h], recv_sem=r1.at[k, h],
            device_id={"pb": to}, device_id_type=MESH,
        )

    def dress(v, k, h, fast=False):
        amp_side = side(amp_perm.at[k], h)
        rows = occ_rows(v, k, h, dot(square[v], amp_side), fast).astype(bf16)
        twice = 2.0 * weight[v]

        def put(i, carry):
            body = (arrived(v, k, h, i).astype(f32) + dot(cols[v, i], amp_side)) * free[...]
            value = (body + dot(pick[i], rows)).astype(bf16)
            term = twice * value.astype(f32) - dot(cols[v, i], rows)
            for s in range(share):
                at = slice(s * LANE, (s + 1) * LANE)
                d[v, k, h * share + s, i] = value[:, at]
                if v == 0:
                    total[h * share + s, i] = term[:, at]
                else:
                    mine = total[h * share + s, i] + term[:, at]
                    for m in range(n):
                        part[k, h, s, i * n + m] = mine[m * rw : (m + 1) * rw].astype(bf16)
            if v:
                for e in range(1, B):
                    to_half(k, h, e, i).start()
            return carry

        loop(put, 0, fast)

    def unpermute(v):
        def one(i, carry):
            natural = []
            for j in range(C):
                ordered = jnp.concatenate([d[v, k, j, i] for k in range(3)], axis=1)
                natural.append(dot(ordered, back[...]))
            dressed[v, pl.ds(pl.multiple_of(i * th, 8), th), :] = jnp.concatenate(natural, axis=1).astype(bf16)
            return carry

        lax.fori_loop(0, C, one, 0)

    cut = (rw // 2 + 7) // 8 * 8
    whole = (pl.ds(0, rw),)
    halves = (pl.ds(0, cut), pl.ds(cut, rw - cut))

    def to_row(k, h, e, at, q):
        return pltpu.make_async_remote_copy(
            src_ref=half.at[k, h, e, at], dst_ref=got2.at[k, h, e, at], send_sem=s2.at[k, h], recv_sem=r2.at[k, h, q],
            device_id={"row": lax.rem(r + e, R)}, device_id_type=MESH,
        )

    def to_col(kind, k, h, at, q):
        mode = {NEAR: 1, PAIR: 1 if k in EARLY else share + 1, FAR: share}[kind]
        return pltpu.make_async_remote_copy(
            src_ref=block.at[k, h, at], dst_ref=got3.at[k, kind, at], send_sem=s3.at[k, kind], recv_sem=r3.at[k, kind, q],
            device_id={"col": peer(c, mode, C)}, device_id_type=MESH,
        )

    def to_pb(k, e, at, q):
        return pltpu.make_async_remote_copy(
            src_ref=final.at[k, at], dst_ref=final.at[k, at], send_sem=s4.at[k], recv_sem=r4.at[k, q],
            device_id={"pb": lax.rem(b + e, B)}, device_id_type=MESH,
        )

    def sum_half(k, h, cuts):
        bytes_of(got1.at[k, h], r1.at[k, h]).wait()
        for q, at in enumerate(cuts):
            for e in list(range(1, R)) + [0]:
                row = lax.rem(r + e, R)
                value = part[k, h, b, row, at].astype(f32)
                for p in range(B - 1):
                    value = value + got1[k, h, p, row, at].astype(f32)
                half[k, h, e, at] = value.astype(bf16)
                if e:
                    to_row(k, h, e, at, q).start()

    mine = lax.rem(c, share) == b
    away = lax.rem(near + 1, B)

    def pass_on(kind, k, at, q):
        @pl.when(jnp.logical_not(mine))
        def _():
            to_col(kind, k, near if kind == NEAR else away, at, q).start()

    def send_far(k, at, q):
        @pl.when(mine)
        def _():
            if k in EARLY:
                to_col(PAIR, k, away, at, q).wait_recv()
                block[k, away] = (block[k, away].astype(f32) + got3[k, PAIR].astype(f32)).astype(bf16)
            to_col(FAR, k, away, at, q).start()

    def sum_row(k, h, cuts, then=()):
        for q, at in enumerate(cuts):
            bytes_of(got2.at[k, h, pl.ds(1, R - 1), at], r2.at[k, h, q]).wait()
            value = half[k, h, 0, at].astype(f32)
            for e in range(1, R):
                value = value + got2[k, h, e, at].astype(f32)
            block[k, h, at] = value.astype(bf16)
            for step in then:
                step(at, q)

    def sum_col(k, cuts):
        @pl.when(mine)
        def _():
            to_col(NEAR, k, near, whole[0], 0).wait_recv()
            for q, at in enumerate(cuts):
                value = block[k, near, at].astype(f32) + got3[k, NEAR, at].astype(f32)
                for kind in (FAR,) if k in EARLY else (FAR, PAIR):
                    to_col(kind, k, away, at, q).wait_recv()
                    value = value + got3[k, kind, at].astype(f32)
                final[k, at] = value
                for e in range(1, B):
                    to_pb(k, e, at, q).start()

    def take_final(k, cuts):
        @pl.when(jnp.logical_not(mine))
        def _():
            for q, at in enumerate(cuts):
                to_pb(k, 1, at, q).wait_recv()

    def natural_fock(k):
        hi = final[k].astype(bf16)
        lo = (final[k] - hi.astype(f32)).astype(bf16)
        return dot(hi, back[k * LANE : (k + 1) * LANE]) + dot(lo, back[k * LANE : (k + 1) * LANE])

    def open_tail(s, carry):
        row, col = lax.div(s, C), lax.rem(s, C)
        for v, value in enumerate(unpack(wides[s], thins[s], mid, low, rw)):
            x[v, 2, col, row] = value
        return carry

    def dresses(v, k):
        def one(h, carry):
            dress(v, k, h)
            return carry

        lax.fori_loop(0, B, one, 0)

    def each_half(step, k):
        def one(h, carry):
            step(k, h, whole)
            return carry

        lax.fori_loop(0, B, one, 0)

    wait_all((FIRST,))
    release((WIDE, THIN))
    weight = [occupied(v) for v in range(2)]
    dresses(0, 0)
    dresses(1, 0)
    each_half(sum_half, 0)
    wait_all((WIDE, THIN))
    release((A_LAST,))
    lax.fori_loop(0, N, open_tail, 0)
    dresses(0, 2)
    dresses(1, 2)
    each_half(sum_half, 2)
    wait_all((A_LAST,))
    release((B_LAST,))
    dresses(0, 1)
    unpermute(0)
    wait_last(0)
    dress(1, 1, near)
    sum_half(1, near, whole)
    for k in EARLY:
        each_half(sum_row, k)
        pass_on(NEAR, k, whole[0], 0)
        pass_on(PAIR, k, whole[0], 0)
    wait_last(1)
    dress(1, 1, away, True)
    for k in EARLY:
        send_far(k, whole[0], 0)
    sum_row(1, near, whole, [functools.partial(pass_on, NEAR, 1)])
    sum_half(1, away, halves)
    unpermute(1)
    sum_row(1, away, halves, [functools.partial(pass_on, PAIR, 1), functools.partial(send_far, 1)])
    for k in EARLY:
        sum_col(k, whole)
    for k in EARLY:
        take_final(k, whole)
    fock[...] = natural_fock(0) + natural_fock(2)
    sum_col(1, halves)
    take_final(1, halves)
    fock[...] = fock[...] + natural_fock(1)
    for kind in range(5):
        bytes_of(every[kind], send.at[kind]).wait()
    bytes_of(amp_all.at[pl.ds(0, R - 1)], amp_sem.at[0]).wait()
    for k in range(3):
        for h in range(B):
            bytes_of(got1.at[k, h], s1.at[k, h]).wait()
            bytes_of(got2.at[k, h, pl.ds(1, R - 1)], s2.at[k, h]).wait()

        @pl.when(jnp.logical_not(mine))
        def _():
            to_col(NEAR, k, near, whole[0], 0).wait_send()
            to_col(PAIR, k, away, whole[0], 0).wait_send()

        @pl.when(mine)
        def _():
            to_col(FAR, k, away, whole[0], 0).wait_send()
            bytes_of(final.at[pl.ds(0, B - 1)], s4.at[k]).wait()


def finish_kernel(before, fock_in, dressed, fock, sem):
    pieces = sem.shape[0] - 1
    step = dressed.shape[1] // (pieces // 2)
    where = [(v, pl.ds(k * step, step)) for v in range(2) for k in range(pieces // 2)]
    stores = [pltpu.make_async_copy(before.at[w], dressed.at[w], sem.at[p]) for p, w in enumerate(where)]
    stores.append(pltpu.make_async_copy(fock_in, fock, sem.at[pieces]))
    for store in stores:
        store.start()
    for store in stores:
        store.wait()


def local(chol, amplitudes):
    B, R, C = lax.axis_size("pb"), lax.axis_size("row"), lax.axis_size("col")
    q_local, rw, cw = chol.shape
    n = cw // rw
    norb = C * cw
    occ = amplitudes.shape[0]
    groups = rw // SH
    mid = 64
    low = cw - 2 * LANE - mid
    rows = 2 * rw // 7
    share = C // B
    N = R * C
    virtual = np.arange(groups * VG)
    widen = virtual[:, None] // VG * SH + OG + virtual[:, None] % VG == np.arange(rw)[None, :]
    index = np.arange(occ)
    place = np.arange(norb)[:, None] == (index // OG * SH + index % OG)[None, :]
    place = place.reshape(C, cw, occ)
    column = np.arange(cw)
    order = np.concatenate([column[column % SH < OG], column[column % SH >= OG]])
    perm = np.zeros((cw, 3 * LANE), bool)
    perm[order, np.arange(cw)] = True
    per_block = occ // C
    occ_of = np.zeros((C, LANE, occ), bool)
    for j in range(C):
        occ_of[j, np.arange(per_block), j * per_block + np.arange(per_block)] = True
    occ_of = occ_of.reshape(B, share * LANE, occ)
    const = lambda array: jnp.asarray(array, bf16)
    hbm = pl.BlockSpec(memory_space=pl.ANY)
    vmem = pl.BlockSpec(memory_space=pltpu.VMEM)
    dma = pltpu.SemaphoreType.DMA
    half_width = lambda *shape: pltpu.VMEM(shape, bf16)
    full_width = lambda *shape: pltpu.VMEM(shape, f32)
    tables = [perm, widen, perm.T, place, place.transpose(0, 2, 1), occ_of]
    tables = [const(array) for array in tables]
    room = lambda array: half_width(*array.shape)
    before, fock_in = pl.pallas_call(
        functools.partial(main_kernel, B, R, C, n, mid, low, rows),
        out_shape=(pltpu.VMEM((2, norb, norb), bf16), pltpu.VMEM((rw, cw), f32)),
        in_specs=[hbm] * (2 + len(tables)),
        out_specs=(vmem, vmem),
        scratch_shapes=[
            half_width(SLOTS, 2, rw, cw),
            half_width(N, 2, 2, rw, LANE),
            half_width(N, rw, LANE),
            half_width(N, rows, LANE),
            half_width(N, rw, LANE),
            half_width(N, rows, LANE),
            half_width(2, 3, C, R, rw, LANE),
            full_width(C, C, cw, LANE),
            half_width(occ, rw),
            half_width(R, occ, rw),
            half_width(C, occ, cw),
            half_width(3, C, occ, LANE),
            half_width(2, C, cw, occ),
            half_width(2, occ, occ),
            full_width(cw, share * LANE),
            half_width(3, B, share, R, rw, LANE),
            half_width(3, B, B - 1, R, rw, LANE),
            half_width(3, B, R, rw, LANE),
            half_width(3, B, R, rw, LANE),
            half_width(3, B, rw, LANE),
            half_width(3, 3, rw, LANE),
            full_width(3, rw, LANE),
            room(tables[0]),
            room(amplitudes),
            *[room(array) for array in tables[1:]],
            dma((5,)), dma((4,)), dma((B,)), dma((2,)), dma((SLOTS,)), dma((1 + len(tables),)),
            dma((3, B)), dma((3, B)), dma((3, B)), dma((3, B, 2)), dma((3, 3)), dma((3, 3, 2)), dma((3,)), dma((3, 2)),
            *([half_width(2, 3, C, C, cw, LANE)] if n > 1 else []),
        ],
        compiler_params=pltpu.CompilerParams(
            collective_id=0, has_side_effects=True, vmem_limit_bytes=MAIN_VMEM
        ),
        name="exchange",
    )(chol, amplitudes, *tables)
    return pl.pallas_call(
        finish_kernel,
        out_shape=(
            jax.ShapeDtypeStruct((2, norb, norb), bf16),
            jax.ShapeDtypeStruct((rw, cw), f32),
        ),
        in_specs=[vmem, vmem],
        out_specs=(hbm, hbm),
        scratch_shapes=[dma((2 * C + 1,))],
        compiler_params=pltpu.CompilerParams(vmem_limit_bytes=16 * 1024 * 1024),
        name="finish",
    )(before, fock_in)


def solution(mesh):
    return jax.shard_map(
        local,
        mesh=mesh,
        in_specs=(P("pb", "row", "col"), P(None, "row")),
        out_specs=(P(("pb", "row", "col"), None, None), P("row", "col")),
        check_vma=False,
    )
```

time: 191 us -> 184 us (0.963)
  Pallas kernels: 191 us -> 183 us
    pallas_call x1, Pallas kernels: 187 us -> 180 us  [local(): pl.pallas_call(functools.partial(main_kernel, B, R, C, n, mid, low, rows)...]
where the time goes in v3:
time: 184 us
  Pallas kernels  183 us (99%)
    pallas_call x1, Pallas kernels, local(): pl.pallas_call(functools.partial(main_kernel, B, R, C, n, mid, low, rows)...  180 us

profile of v3, /device:TPU:1, one launch (start us, length us, event | category | flops | bytes accessed | tf_op | source)
XLA Modules:
  0.0 183.5 jit_solution(18243311820790980952)
XLA Ops:
  0.6 179.6 %exchange.1 = (bf16[2,1344,1344]{2,1,0:T(8,128)(2,1)S(1)}, f32[336,336]{1,0:T(8,128)S(1)}) custom-call(bf16[32,336,336]{2,1,0:T(8,128)(2,1)} %chol.1, bf16[144,300]{1,0:T(8,128)(2,1)} %amp_in.1, bf16[336,384]{1,0:T(8,128)(2,1)} %constant.12.clone.perm_in, bf16[300,336]{1,0:T(8,128)(2,1)} %constant.13.clone.widen_in, ...), custom_call_target="tpu_custom_call" | custom-call | tf_op jit(solution)/shard_map/exchange/pallas_call | solution.py:513
  180.2 3.3 %finish.1 = (bf16[2,1344,1344]{2,1,0:T(8,128)(2,1)}, f32[336,336]{1,0:T(8,128)}) custom-call(bf16[2,1344,1344]{2,1,0:T(8,128)(2,1)S(1)} %get-tuple-element.4.before, f32[336,336]{1,0:T(8,128)S(1)} %get-tuple-element.5.fock_in), custom_call_target="tpu_custom_call" | custom-call | tf_op jit(solution)/shard_map/finish/pallas_call | solution.py:553

commit v4 on v3

--- a/solution.py
+++ b/solution.py
@@ -35,7 +35,6 @@
     wide = jnp.concatenate([first[:, :mid], second[:, :mid]], axis=1).astype(bf16)
     thin = jnp.concatenate([first[:, mid:], second[:, mid:]], axis=0)
     pieces = [thin[k * rows : (k + 1) * rows] for k in range(thin.shape[0] // rows)]
-    pieces.append(jnp.zeros((rows, LANE - low * len(pieces)), f32))
     return wide, jnp.concatenate(pieces, axis=1).astype(bf16)
 
 
@@ -59,10 +58,10 @@
 
 def main_kernel(
     B, R, C, n, mid, low, rows, chol, amp_in, perm_in, widen_in, back_in, pick_in, pick_t_in, occ_of_in,
-    dressed, fock,
+    dressed, final, back,
     stage, packed, wide_out, thin_out, wides, thins, x, total, amp_out, amp_all, joint, amp_perm, cols, square, free,
-    part, got1, half, got2, block, got3, final, perm, amp, widen, back, pick, pick_t, occ_of,
-    send, recv, recv_last, amp_sem, load, table, s1, r1, s2, r2, s3, r3, s4, r4, *taller,
+    part, got1, half, got2, block, got3, perm, amp, widen, pick, pick_t, occ_of,
+    send, recv, recv_last, amp_sem, load, table, s1, r1, r1_last, s2, r2, s3, r3, s4, r4, *taller,
 ):
     d = taller[0] if taller else x
     b, r, c = lax.axis_index("pb"), lax.axis_index("row"), lax.axis_index("col")
@@ -72,6 +71,8 @@
     rw, cw = chol.shape[1], chol.shape[2]
     th = rw * n
     near = lax.div(c, share)
+    mine = lax.rem(c, share) == b
+    away = lax.rem(near + 1, B)
 
     def place(m):
         k = lax.rem(lax.div(m, 2) + lax.rem(m, 2), N // 2)
@@ -83,18 +84,18 @@
         slot = lax.rem(m, SLOTS)
         return pltpu.make_async_copy(chol.at[pl.ds((row * C + col) * 2, 2)], stage.at[slot], load.at[slot])
 
+    tables = [(perm_in, perm), (amp_in, amp), (widen_in, widen), (back_in, back),
+              (pick_in, pick), (pick_t_in, pick_t), (occ_of_in, occ_of)]
+    tables = [pltpu.make_async_copy(src, dst, table.at[i]) for i, (src, dst) in enumerate(tables)]
+    tables[0].start()
+    for m in range(SLOTS):
+        fetch(m).start()
     barrier = pltpu.get_barrier_semaphore()
     for m in range(N - 1):
         row, col = place(m)
         pl.semaphore_signal(barrier, inc=1, device_id={"row": row, "col": col}, device_id_type=MESH)
     for e in range(1, B):
         pl.semaphore_signal(barrier, inc=1, device_id={"pb": lax.rem(b + e, B)}, device_id_type=MESH)
-    tables = [(perm_in, perm), (amp_in, amp), (widen_in, widen), (back_in, back),
-              (pick_in, pick), (pick_t_in, pick_t), (occ_of_in, occ_of)]
-    tables = [pltpu.make_async_copy(src, dst, table.at[i]) for i, (src, dst) in enumerate(tables)]
-    tables[0].start()
-    for m in range(SLOTS):
-        fetch(m).start()
     tables[0].wait()
 
     def bytes_of(ref, sem):
@@ -257,19 +258,20 @@
         diag = jnp.where(on, corner.astype(f32), 0.0)
         return jnp.sum(jnp.sum(diag, axis=1, keepdims=True), axis=0, keepdims=True)
 
-    def to_half(k, h, e, i):
+    def to_half(k, h, e, i, sem):
         to, of = lax.rem(b + e, B), pl.ds(i * n, n)
         return pltpu.make_async_remote_copy(
-            src_ref=part.at[k, h, to, of], dst_ref=got1.at[k, h, e - 1, of], send_sem=s1.at[k, h], recv_sem=r1.at[k, h],
+            src_ref=part.at[k, h, to, of], dst_ref=got1.at[k, h, e - 1, of], send_sem=s1.at[k, h], recv_sem=sem,
             device_id={"pb": to}, device_id_type=MESH,
         )
 
-    def dress(v, k, h, fast=False):
+    def dress(v, k, h, then=None):
+        fast = then is not None
         amp_side = side(amp_perm.at[k], h)
         rows = occ_rows(v, k, h, dot(square[v], amp_side), fast).astype(bf16)
         twice = 2.0 * weight[v]
 
-        def put(i, carry):
+        def put(i, sem):
             body = (arrived(v, k, h, i).astype(f32) + dot(cols[v, i], amp_side)) * free[...]
             value = (body + dot(pick[i], rows)).astype(bf16)
             term = twice * value.astype(f32) - dot(cols[v, i], rows)
@@ -284,12 +286,23 @@
                         part[k, h, s, i * n + m] = mine[m * rw : (m + 1) * rw].astype(bf16)
             if v:
                 for e in range(1, B):
-                    to_half(k, h, e, i).start()
+                    to_half(k, h, e, i, sem).start()
+
+        def one(i, carry):
+            put(i, r1.at[k, h])
             return carry
 
-        loop(put, 0, fast)
-
-    def unpermute(v):
+        if not fast:
+            lax.fori_loop(0, C, one, 0)
+            return
+        turns = list(range(1, C)) + [0]
+        for number, turn in enumerate(turns):
+            put(lax.rem(lax.div(r, n) + turn, C), r1_last.at[turn])
+            if number:
+                then(turns[number - 1])
+        then(turns[-1])
+
+    def unpermute(v, first=0, last=C):
         def one(i, carry):
             natural = []
             for j in range(C):
@@ -298,7 +311,7 @@
             dressed[v, pl.ds(pl.multiple_of(i * th, 8), th), :] = jnp.concatenate(natural, axis=1).astype(bf16)
             return carry
 
-        lax.fori_loop(0, C, one, 0)
+        lax.fori_loop(first, last, one, 0)
 
     cut = (rw // 2 + 7) // 8 * 8
     whole = (pl.ds(0, rw),)
@@ -335,8 +348,22 @@
                 if e:
                     to_row(k, h, e, at, q).start()
 
-    mine = lax.rem(c, share) == b
-    away = lax.rem(near + 1, B)
+    def sum_block(turn):
+        i = lax.rem(lax.div(r, n) + turn, C)
+        bytes_of(got1.at[1, away, :, pl.ds(i * n, n)], r1_last.at[turn]).wait()
+        for m in range(n):
+            row = i * n + m
+            e = lax.rem(row - r + R, R)
+            value = part[1, away, b, row].astype(f32)
+            for p in range(B - 1):
+                value = value + got1[1, away, p, row].astype(f32)
+            half[1, away, e] = value.astype(bf16)
+            if n > 1 or turn:
+                @pl.when(e != 0)
+                def _():
+                    for q, at in enumerate(halves):
+                        to_row(1, away, e, at, q).start()
+
 
     def pass_on(kind, k, at, q):
         @pl.when(jnp.logical_not(mine))
@@ -379,11 +406,6 @@
         def _():
             for q, at in enumerate(cuts):
                 to_pb(k, 1, at, q).wait_recv()
-
-    def natural_fock(k):
-        hi = final[k].astype(bf16)
-        lo = (final[k] - hi.astype(f32)).astype(bf16)
-        return dot(hi, back[k * LANE : (k + 1) * LANE]) + dot(lo, back[k * LANE : (k + 1) * LANE])
 
     def open_tail(s, carry):
         row, col = lax.div(s, C), lax.rem(s, C)
@@ -421,29 +443,27 @@
     release((B_LAST,))
     dresses(0, 1)
     unpermute(0)
-    wait_last(0)
-    dress(1, 1, near)
-    sum_half(1, near, whole)
     for k in EARLY:
         each_half(sum_row, k)
         pass_on(NEAR, k, whole[0], 0)
         pass_on(PAIR, k, whole[0], 0)
+    wait_last(0)
+    dress(1, 1, near)
+    sum_half(1, near, whole)
     wait_last(1)
-    dress(1, 1, away, True)
     for k in EARLY:
         send_far(k, whole[0], 0)
+    dress(1, 1, away, sum_block)
     sum_row(1, near, whole, [functools.partial(pass_on, NEAR, 1)])
-    sum_half(1, away, halves)
-    unpermute(1)
+    unpermute(1, 0, C // 2)
     sum_row(1, away, halves, [functools.partial(pass_on, PAIR, 1), functools.partial(send_far, 1)])
+    unpermute(1, C // 2, C)
     for k in EARLY:
         sum_col(k, whole)
+    sum_col(1, halves)
     for k in EARLY:
         take_final(k, whole)
-    fock[...] = natural_fock(0) + natural_fock(2)
-    sum_col(1, halves)
     take_final(1, halves)
-    fock[...] = fock[...] + natural_fock(1)
     for kind in range(5):
         bytes_of(every[kind], send.at[kind]).wait()
     bytes_of(amp_all.at[pl.ds(0, R - 1)], amp_sem.at[0]).wait()
@@ -463,14 +483,22 @@
             bytes_of(final.at[pl.ds(0, B - 1)], s4.at[k]).wait()
 
 
-def finish_kernel(before, fock_in, dressed, fock, sem):
+def finish_kernel(before, final, back, dressed, fock, natural, sem):
     pieces = sem.shape[0] - 1
     step = dressed.shape[1] // (pieces // 2)
     where = [(v, pl.ds(k * step, step)) for v in range(2) for k in range(pieces // 2)]
     stores = [pltpu.make_async_copy(before.at[w], dressed.at[w], sem.at[p]) for p, w in enumerate(where)]
-    stores.append(pltpu.make_async_copy(fock_in, fock, sem.at[pieces]))
     for store in stores:
         store.start()
+    value = jnp.zeros(natural.shape, f32)
+    for k in range(3):
+        hi = final[k].astype(bf16)
+        lo = (final[k] - hi.astype(f32)).astype(bf16)
+        table = back[k * LANE : (k + 1) * LANE]
+        value = value + dot(hi, table) + dot(lo, table)
+    natural[...] = value
+    stores.append(pltpu.make_async_copy(natural, fock, sem.at[pieces]))
+    stores[-1].start()
     for store in stores:
         store.wait()
 
@@ -484,7 +512,7 @@
     groups = rw // SH
     mid = 64
     low = cw - 2 * LANE - mid
-    rows = 2 * rw // 7
+    rows = 2 * rw * low // LANE
     share = C // B
     N = R * C
     virtual = np.arange(groups * VG)
@@ -510,11 +538,15 @@
     tables = [perm, widen, perm.T, place, place.transpose(0, 2, 1), occ_of]
     tables = [const(array) for array in tables]
     room = lambda array: half_width(*array.shape)
-    before, fock_in = pl.pallas_call(
+    before, final, back = pl.pallas_call(
         functools.partial(main_kernel, B, R, C, n, mid, low, rows),
-        out_shape=(pltpu.VMEM((2, norb, norb), bf16), pltpu.VMEM((rw, cw), f32)),
+        out_shape=(
+            pltpu.VMEM((2, norb, norb), bf16),
+            pltpu.VMEM((3, rw, LANE), f32),
+            pltpu.VMEM(tables[2].shape, bf16),
+        ),
         in_specs=[hbm] * (2 + len(tables)),
-        out_specs=(vmem, vmem),
+        out_specs=(vmem, vmem, vmem),
         scratch_shapes=[
             half_width(SLOTS, 2, rw, cw),
             half_width(N, 2, 2, rw, LANE),
@@ -537,12 +569,12 @@
             half_width(3, B, R, rw, LANE),
             half_width(3, B, rw, LANE),
             half_width(3, 3, rw, LANE),
-            full_width(3, rw, LANE),
             room(tables[0]),
             room(amplitudes),
-            *[room(array) for array in tables[1:]],
+            room(tables[1]),
+            *[room(array) for array in tables[3:]],
             dma((5,)), dma((4,)), dma((B,)), dma((2,)), dma((SLOTS,)), dma((1 + len(tables),)),
-            dma((3, B)), dma((3, B)), dma((3, B)), dma((3, B, 2)), dma((3, 3)), dma((3, 3, 2)), dma((3,)), dma((3, 2)),
+            dma((3, B)), dma((3, B)), dma((C,)), dma((3, B)), dma((3, B, 2)), dma((3, 3)), dma((3, 3, 2)), dma((3,)), dma((3, 2)),
             *([half_width(2, 3, C, C, cw, LANE)] if n > 1 else []),
         ],
         compiler_params=pltpu.CompilerParams(
@@ -556,12 +588,12 @@
             jax.ShapeDtypeStruct((2, norb, norb), bf16),
             jax.ShapeDtypeStruct((rw, cw), f32),
         ),
-        in_specs=[vmem, vmem],
+        in_specs=[vmem, vmem, vmem],
         out_specs=(hbm, hbm),
-        scratch_shapes=[dma((2 * C + 1,))],
+        scratch_shapes=[full_width(rw, cw), dma((2 * C + 1,))],
         compiler_params=pltpu.CompilerParams(vmem_limit_bytes=16 * 1024 * 1024),
         name="finish",
-    )(before, fock_in)
+    )(before, final, back)
 
 
 def solution(mesh):

time: 184 us -> 183 us (level)
  no operation moved by 1% of the time
where the time goes in v4:
time: 183 us
  Pallas kernels  182 us (99%)
    pallas_call x1, Pallas kernels, local(): pl.pallas_call(functools.partial(main_kernel, B, R, C, n, mid, low, rows)...  179 us

profile of v4, /device:TPU:1, one launch (start us, length us, event | category | flops | bytes accessed | tf_op | source)
XLA Modules:
  0.0 182.7 jit_solution(6793291523725579252)
XLA Ops:
  0.6 178.8 %exchange.1 = (bf16[2,1344,1344]{2,1,0:T(8,128)(2,1)S(1)}, f32[3,336,128]{2,1,0:T(8,128)S(1)}, bf16[384,336]{1,0:T(8,128)(2,1)S(1)}) custom-call(bf16[32,336,336]{2,1,0:T(8,128)(2,1)} %chol.1, bf16[144,300]{1,0:T(8,128)(2,1)} %amp_in.1, bf16[336,384]{1,0:T(8,128)(2,1)} %constant.12.clone.perm_in, bf16[300,336]{1,0:T(8,128)(2,1)} %constant.13.clone.widen_in, ...), custom_call_target="tpu_custom_call" | custom-call | tf_op jit(solution)/shard_map/exchange/pallas_call | solution.py:541
  179.5 3.3 %finish.1 = (bf16[2,1344,1344]{2,1,0:T(8,128)(2,1)}, f32[336,336]{1,0:T(8,128)}) custom-call(bf16[2,1344,1344]{2,1,0:T(8,128)(2,1)S(1)} %get-tuple-element.5.before, f32[3,336,128]{2,1,0:T(8,128)S(1)} %get-tuple-element.6.final, bf16[384,336]{1,0:T(8,128)(2,1)S(1)} %get-tuple-element.7.back), custom_call_target="tpu_custom_call" | custom-call | tf_op jit(solution)/shard_map/finish/pallas_call | solution.py:585

commit v5 on v4

v5 whole, which is shorter than its diff:
```python
import functools
import jax
import numpy as np
import jax.numpy as jnp
from jax import lax
from jax.experimental import pallas as pl
from jax.experimental.pallas import tpu as pltpu
from jax.sharding import PartitionSpec as P

OG = 9
VG = 75
SH = 84
LANE = 128
MESH = pl.DeviceIdType.MESH
f32, bf16 = jnp.float32, jnp.bfloat16


def dot(a, b):
    return jnp.dot(a, b, preferred_element_type=f32)


def peer(index, mode, size):
    if size & (size - 1):
        return lax.rem(index + mode, size)
    bits = [1 << k for k in range(size.bit_length() - 1)]
    flip = lambda bit: lax.rem(lax.rem(lax.div(index, bit), 2) + lax.rem(lax.div(mode, bit), 2), 2) * bit
    return sum(flip(bit) for bit in bits)


def lanes(parts):
    return jnp.concatenate([p.astype(f32) for p in parts], axis=1).astype(bf16)


def pack(first, second, mid, low, rows):
    wide = jnp.concatenate([first[:, :mid], second[:, :mid]], axis=1).astype(bf16)
    thin = jnp.concatenate([first[:, mid:], second[:, mid:]], axis=0)
    pieces = [thin[k * rows : (k + 1) * rows] for k in range(thin.shape[0] // rows)]
    return wide, jnp.concatenate(pieces, axis=1).astype(bf16)


def unpack(thin, low, rw):
    thin = thin.astype(f32)
    rows = thin.shape[0]
    pieces = [thin[:, k * low : (k + 1) * low] for k in range(2 * rw // rows)]
    thin = jnp.concatenate(pieces, axis=0)
    blank = jnp.zeros((rw, LANE - low), f32)
    for v in range(2):
        yield jnp.concatenate([thin[v * rw : (v + 1) * rw], blank], axis=1).astype(bf16)


SLOTS = 4
MAIN_VMEM = 54 * 1024 * 1024
FIRST, MID_A, MID_B, THIN, WIDE = range(5)
NEAR, PAIR, FAR = range(3)
EARLY = (0, 1, 2)
LATE = 3


def main_kernel(
    B, R, C, n, mid, low, rows, spans, chol, amp_in, perm_in, widen_in, order_in, back_in, pick_in, occ_of_in, wide_back_in,
    dressed, final, final_late, back,
    stage, packed, wide_out, thin_out, wides, thins, x, total, amp_out, amp_all, joint, amp_perm, cols, square, free, ahead,
    part, got1, half, got2, block, got3, part_late, got1_late, half_late, got2_late, block_late, got3_late,
    perm, amp, widen, order, pick, occ_of, wide_back,
    send, recv, recv_last, amp_sem, load, table, s1, r1, r1_last, s2, r2, s3, r3, s4, r4, *taller,
):
    d = taller[0] if taller else x
    wide_d = taller[1] if taller else wides
    b, r, c = lax.axis_index("pb"), lax.axis_index("row"), lax.axis_index("col")
    me = r * C + c
    N = R * C
    share = C // B
    rw, cw = chol.shape[1], chol.shape[2]
    th = rw * n
    near = lax.div(c, share)
    mine = lax.rem(c, share) == b
    away = lax.rem(near + 1, B)

    def place(m):
        k = lax.rem(lax.div(m, 2) + lax.rem(m, 2), N // 2)
        dc = lax.rem(k, C // 2) + (C // 2) * (1 - lax.rem(m, 2))
        return peer(r, lax.div(k, C // 2), R), peer(c, dc, C)

    def fetch(m):
        row, col = place(m)
        slot = lax.rem(m, SLOTS)
        return pltpu.make_async_copy(chol.at[pl.ds((row * C + col) * 2, 2)], stage.at[slot], load.at[slot])

    tables = [(perm_in, perm), (amp_in, amp), (widen_in, widen), (order_in, order), (back_in, back),
              (pick_in, pick), (occ_of_in, occ_of), (wide_back_in, wide_back)]
    tables = [pltpu.make_async_copy(src, dst, table.at[i]) for i, (src, dst) in enumerate(tables)]
    tables[0].start()
    for m in range(SLOTS):
        fetch(m).start()
    barrier = pltpu.get_barrier_semaphore()
    for m in range(N - 1):
        row, col = place(m)
        pl.semaphore_signal(barrier, inc=1, device_id={"row": row, "col": col}, device_id_type=MESH)
    for e in range(1, B):
        pl.semaphore_signal(barrier, inc=1, device_id={"pb": lax.rem(b + e, B)}, device_id_type=MESH)
    tables[0].wait()

    def bytes_of(ref, sem):
        return pltpu.make_async_copy(ref, ref, sem)

    others = pl.ds(0, N - 1)
    every = {
        FIRST: packed.at[others, pl.ds(0, 2), 0],
        MID_A: packed.at[others, 0, 1],
        MID_B: packed.at[others, 1, 1],
        THIN: thin_out.at[others],
        WIDE: wide_out.at[others],
    }

    def move(kind, m):
        row, col = place(m)
        src, dst = {
            FIRST: (packed.at[m, pl.ds(0, 2), 0], x.at[pl.ds(0, 2), 0, c, r]),
            MID_A: (packed.at[m, 0, 1], x.at[0, 1, c, r]),
            MID_B: (packed.at[m, 1, 1], x.at[1, 1, c, r]),
            THIN: (thin_out.at[m], thins.at[me]),
            WIDE: (wide_out.at[m], wides.at[c, r]),
        }[kind]
        turn = lax.rem(near - lax.div(col, share) + B, B)
        return pltpu.make_async_remote_copy(
            src_ref=src, dst_ref=dst, send_sem=send.at[kind],
            recv_sem=recv_last.at[turn] if kind == WIDE else recv.at[kind],
            device_id={"row": row, "col": col}, device_id_type=MESH,
        )

    def wait_all(kinds):
        for kind in kinds:
            bytes_of(every[kind], recv.at[kind]).wait()

    def wait_last(turn):
        count = R * share - (turn == 0)
        bytes_of(wide_out.at[pl.ds(0, count)], recv_last.at[turn]).wait()

    def order_columns(m):
        fetch(m).wait()
        slot = lax.rem(m, SLOTS)
        tails = []
        for v in range(2):
            y = dot(stage[slot, v], perm[...])
            packed[m, v, 0] = y[:, :LANE].astype(bf16)
            packed[m, v, 1] = y[:, LANE : 2 * LANE].astype(bf16)
            tails.append(y[:, 2 * LANE : 2 * LANE + mid + low])
        return tails

    def pack_tails(m, tails):
        wide, thin = pack(tails[0], tails[1], mid, low, rows)
        wide_out[m] = wide
        thin_out[m] = thin

        @pl.when(m + SLOTS < N)
        def _():
            fetch(m + SLOTS).start()

    def permute(m, carry):
        tails = order_columns(m)

        @pl.when(m < N - 1)
        def _():
            move(FIRST, m).start()

        pack_tails(m, tails)
        return carry

    first_tails = order_columns(0)
    pl.semaphore_wait(barrier, N - 1 + B - 1)
    move(FIRST, 0).start()
    pack_tails(0, first_tails)
    lax.fori_loop(1, N, permute, 0)
    for copy in tables[1:]:
        copy.start()
    for copy in tables[1:]:
        copy.wait()
    own_amp = dot(amp[...], widen[...]).astype(bf16)
    amp_out[...] = own_amp
    amp_all[r] = own_amp

    def amp_move(k):
        return pltpu.make_async_remote_copy(
            src_ref=amp_out, dst_ref=amp_all.at[r], send_sem=amp_sem.at[0], recv_sem=amp_sem.at[1],
            device_id={"row": peer(r, k, R)}, device_id_type=MESH,
        )

    for k in range(1, R):
        amp_move(k).start()

    def start_all(kinds):
        def one(m, carry):
            for kind in kinds:
                move(kind, m).start()
            return carry

        lax.fori_loop(0, N - 1, one, 0)

    inner = (c > 0) & (c < C - 1)

    @pl.when(inner)
    def _():
        for kinds in ((THIN, MID_A), (MID_B,), (WIDE,)):
            start_all(kinds)

    def release(kinds):
        @pl.when(jnp.logical_not(inner))
        def _():
            start_all(kinds)

    for v in range(2):
        for k in range(2):
            x[v, k, c, r] = packed[N - 1, v, k]
    wides[c, r] = wide_out[N - 1]
    thins[me] = thin_out[N - 1]
    ones = jnp.ones((pick.shape[2], share * LANE), bf16)
    free[...] = 1.0 - dot(pick[0], ones)
    bytes_of(amp_all.at[pl.ds(0, R - 1)], amp_sem.at[1]).wait()
    square_of = (pick.shape[2], pick.shape[2])
    on = lax.broadcasted_iota(jnp.int32, square_of, 0) == lax.broadcasted_iota(jnp.int32, square_of, 1)
    eye = jnp.where(on, 1.0, 0.0).astype(bf16)
    for i in range(C):
        whole = amp_all[i] if n == 1 else lanes([amp_all[i * n + m] for m in range(n)])
        turned = lax.dot_general(eye, pick[i], (((1,), (1,)), ((), ())), preferred_element_type=f32)
        joint[i] = (turned - whole.astype(f32)).astype(bf16)
        ordered = dot(whole, order[...]).astype(bf16)
        for k in range(4):
            amp_perm[k, i] = ordered[:, k * LANE : (k + 1) * LANE]

    def side(ref, h):
        return jnp.concatenate([ref[h * share + s] for s in range(share)], axis=1)

    def arrived(v, k, h, i):
        if n == 1:
            return side(x.at[v, k, :, i], h)
        tall = [side(x.at[v, k, :, i * n + m], h).astype(f32) for m in range(n)]
        return jnp.concatenate(tall, axis=0).astype(bf16)

    def loop(body, start, fast):
        if not fast:
            return lax.fori_loop(0, C, body, start)
        for i in range(C):
            start = body(i, start)
        return start

    def occ_rows(v, k, h, start, fast=False):
        return loop(lambda i, rows: rows + dot(joint[i], arrived(v, k, h, i)), start, fast)

    def occupied(v):
        blank = jnp.zeros((joint.shape[1], share * LANE), f32)
        block_of = sum(dot(occ_rows(v, 0, h, blank).astype(bf16), occ_of[h]) for h in range(B))
        square[v] = block_of.astype(bf16)
        corner = block_of.astype(bf16)

        def one(i, carry):
            virtual = sum(dot(arrived(v, 0, h, i), occ_of[h]) for h in range(B)) * free[:, : virtual_width]
            cols[v, i] = (virtual + dot(pick[i], corner)).astype(bf16)
            return carry

        virtual_width = corner.shape[1]
        lax.fori_loop(0, C, one, 0)
        diag = jnp.where(on, corner.astype(f32), 0.0)
        return jnp.sum(jnp.sum(diag, axis=1, keepdims=True), axis=0, keepdims=True)

    late_rows = part_late.shape[3]
    late = (part_late, got1_late, half_late, got2_late, block_late, got3_late, final_late)
    early = (part, got1, half, got2, block, got3, final)

    def of(which, k):
        return late[which] if k == LATE else early[which].at[k]

    PART, GOT1, HALF, GOT2, BLOCK, GOT3, FINAL = range(7)

    def to_half(k, h, e, i, sem):
        to, at = lax.rem(b + e, B), pl.ds(i * n, n)
        return pltpu.make_async_remote_copy(
            src_ref=of(PART, k).at[h, to, at], dst_ref=of(GOT1, k).at[h, e - 1, at], send_sem=s1.at[k, h], recv_sem=sem,
            device_id={"pb": to}, device_id_type=MESH,
        )

    def dress(v, k, h):
        amp_side = side(amp_perm.at[k], h)
        rows = occ_rows(v, k, h, dot(square[v], amp_side)).astype(bf16)
        twice = 2.0 * weight[v]

        def put(i, carry):
            body = (arrived(v, k, h, i).astype(f32) + dot(cols[v, i], amp_side)) * free[...]
            value = (body + dot(pick[i], rows)).astype(bf16)
            term = twice * value.astype(f32) - dot(cols[v, i], rows)
            for s in range(share):
                at = slice(s * LANE, (s + 1) * LANE)
                d[v, k, h * share + s, i] = value[:, at]
                if v == 0:
                    total[h * share + s, i] = term[:, at]
                else:
                    mine = total[h * share + s, i] + term[:, at]
                    for m in range(n):
                        part[k, h, s, i * n + m] = mine[m * rw : (m + 1) * rw].astype(bf16)
            if v:
                for e in range(1, B):
                    to_half(k, h, e, i, r1.at[k, h]).start()
            return carry

        lax.fori_loop(0, C, put, 0)

    def lane_of(width):
        return lax.rem(lax.broadcasted_iota(jnp.int32, (1, width), 1), LANE) < mid

    def wide_side(h, i):
        if n == 1:
            return side(wides.at[:, i], h)
        tall = [side(wides.at[:, i * n + m], h).astype(f32) for m in range(n)]
        return jnp.concatenate(tall, axis=0).astype(bf16)

    def prepare_late(h):
        amp_side = side(amp_perm.at[LATE], h)
        first = lane_of(share * LANE)

        def one(i, carry):
            ahead[i] = jnp.where(first, dot(cols[0, i], amp_side), dot(cols[1, i], amp_side))
            return carry

        lax.fori_loop(0, C, one, 0)

    def dress_late(h, then=None):
        amp_side = side(amp_perm.at[LATE], h)
        first, tile_first = lane_of(share * LANE), lane_of(LANE)
        rows = jnp.where(first, dot(square[0], amp_side), dot(square[1], amp_side))
        rows = loop(lambda i, total_rows: total_rows + dot(joint[i], wide_side(h, i)), rows, then is not None).astype(bf16)
        twice = jnp.where(first, 2.0 * weight[0], 2.0 * weight[1])

        def put(i, sem):
            body = (wide_side(h, i).astype(f32) + ahead[i]) * free[...]
            value = (body + dot(pick[i], rows)).astype(bf16)
            term = twice * value.astype(f32) - jnp.where(first, dot(cols[0, i], rows), dot(cols[1, i], rows))
            for s in range(share):
                at = slice(s * LANE, (s + 1) * LANE)
                wide_d[h * share + s, i] = value[:, at]
                both = term[:, at] + pltpu.roll(term[:, at], mid, 1)
                for m in range(n):
                    upper = both[m * rw : m * rw + late_rows]
                    lower = both[m * rw + late_rows : (m + 1) * rw]
                    short = 2 * late_rows - rw
                    if short:
                        lower = jnp.concatenate([lower, jnp.zeros((short, LANE), f32)], axis=0)
                    part_late[h, s, i * n + m] = jnp.where(tile_first, upper, lower).astype(bf16)
            for e in range(1, B):
                to_half(LATE, h, e, i, sem).start()

        if then is None:
            def one(i, carry):
                put(i, r1.at[LATE, h])
                return carry

            lax.fori_loop(0, C, one, 0)
            return
        turns = list(range(1, C)) + [0]
        for number, turn in enumerate(turns):
            put(lax.rem(lax.div(r, n) + turn, C), r1_last.at[turn])
            if number:
                then(turns[number - 1])
        then(turns[-1])

    def strip(i):
        return pl.ds(pl.multiple_of(i * th, 8), th)

    def unpermute(t, carry):
        v, i = lax.div(t, C), lax.rem(t, C)
        natural = []
        for j in range(C):
            ordered = jnp.concatenate([d[v, k, j, i] for k in range(3)], axis=1)
            natural.append(dot(ordered, back[: 3 * LANE]))
        dressed[v, strip(i), :] = jnp.concatenate(natural, axis=1).astype(bf16)
        return carry

    def unpermute_late(v):
        def one(i, carry):
            for j, (start, stop) in enumerate(spans):
                at = (v, strip(i), slice(start, stop))
                natural = dot(wide_d[j, i], wide_back[j, v][:, : stop - start])
                dressed[at] = (dressed[at].astype(f32) + natural).astype(bf16)
            return carry

        lax.fori_loop(0, C, one, 0)

    cut = (late_rows // 2 + 7) // 8 * 8
    whole = (pl.ds(0, rw),)
    late_whole = (pl.ds(0, late_rows),)
    halves = (pl.ds(0, cut), pl.ds(cut, late_rows - cut))

    def all_of(k):
        return late_whole if k == LATE else whole

    def to_row(k, h, e, at, q):
        return pltpu.make_async_remote_copy(
            src_ref=of(HALF, k).at[h, e, at], dst_ref=of(GOT2, k).at[h, e, at], send_sem=s2.at[k, h],
            recv_sem=r2.at[k, h, q], device_id={"row": lax.rem(r + e, R)}, device_id_type=MESH,
        )

    def to_col(kind, k, h, at, q):
        mode = {NEAR: 1, PAIR: 1 if k in EARLY else share + 1, FAR: share}[kind]
        return pltpu.make_async_remote_copy(
            src_ref=of(BLOCK, k).at[h, at], dst_ref=of(GOT3, k).at[kind, at], send_sem=s3.at[k, kind],
            recv_sem=r3.at[k, kind, q], device_id={"col": peer(c, mode, C)}, device_id_type=MESH,
        )

    def to_pb(k, e, at, q):
        return pltpu.make_async_remote_copy(
            src_ref=of(FINAL, k).at[at], dst_ref=of(FINAL, k).at[at], send_sem=s4.at[k], recv_sem=r4.at[k, q],
            device_id={"pb": lax.rem(b + e, B)}, device_id_type=MESH,
        )

    def sum_half(k, h, cuts):
        mine_part, got, out = of(PART, k), of(GOT1, k), of(HALF, k)
        bytes_of(got.at[h], r1.at[k, h]).wait()
        for e in list(range(1, R)) + [0]:
            row = lax.rem(r + e, R)
            value = mine_part[h, b, row].astype(f32)
            for p in range(B - 1):
                value = value + got[h, p, row].astype(f32)
            out[h, e] = value.astype(bf16)
            if e:
                to_row(k, h, e, cuts[0], 0).start()

    def sum_block(turn):
        i = lax.rem(lax.div(r, n) + turn, C)
        bytes_of(got1_late.at[away, :, pl.ds(i * n, n)], r1_last.at[turn]).wait()
        for m in range(n):
            row = i * n + m
            e = lax.rem(row - r + R, R)
            value = part_late[away, b, row].astype(f32)
            for p in range(B - 1):
                value = value + got1_late[away, p, row].astype(f32)
            half_late[away, e] = value.astype(bf16)
            if n > 1 or turn:
                @pl.when(e != 0)
                def _():
                    for q, at in enumerate(halves):
                        to_row(LATE, away, e, at, q).start()

    def pass_on(kind, k, at, q):
        @pl.when(jnp.logical_not(mine))
        def _():
            to_col(kind, k, near if kind == NEAR else away, at, q).start()

    def send_far(k, at, q):
        out, got = of(BLOCK, k), of(GOT3, k)

        @pl.when(mine)
        def _():
            if k in EARLY:
                to_col(PAIR, k, away, at, q).wait_recv()
                out[away] = (out[away].astype(f32) + got[PAIR].astype(f32)).astype(bf16)
            to_col(FAR, k, away, at, q).start()

    def sum_row(k, h, cuts, then=()):
        own, got, out = of(HALF, k), of(GOT2, k), of(BLOCK, k)
        for q, at in enumerate(cuts):
            bytes_of(got.at[h, pl.ds(1, R - 1), at], r2.at[k, h, q]).wait()
            value = own[h, 0, at].astype(f32)
            for e in range(1, R):
                value = value + got[h, e, at].astype(f32)
            out[h, at] = value.astype(bf16)
            for step in then:
                step(at, q)

    def sum_col(k, cuts):
        own, got, out = of(BLOCK, k), of(GOT3, k), of(FINAL, k)

        @pl.when(mine)
        def _():
            to_col(NEAR, k, near, all_of(k)[0], 0).wait_recv()
            for q, at in enumerate(cuts):
                value = own[near, at].astype(f32) + got[NEAR, at].astype(f32)
                for kind in (FAR,) if k in EARLY else (FAR, PAIR):
                    to_col(kind, k, away, at, q).wait_recv()
                    value = value + got[kind, at].astype(f32)
                out[at] = value
                for e in range(1, B):
                    to_pb(k, e, at, q).start()

    def take_final(k, cuts):
        @pl.when(jnp.logical_not(mine))
        def _():
            for q, at in enumerate(cuts):
                to_pb(k, 1, at, q).wait_recv()

    def open_tail(s, carry):
        row, col = lax.div(s, C), lax.rem(s, C)
        for v, value in enumerate(unpack(thins[s], low, rw)):
            x[v, 2, col, row] = value
        return carry

    def dresses(v, k):
        def one(h, carry):
            dress(v, k, h)
            return carry

        lax.fori_loop(0, B, one, 0)

    def each_half(step, k):
        def one(h, carry):
            step(k, h, whole)
            return carry

        lax.fori_loop(0, B, one, 0)

    wait_all((FIRST,))
    release((THIN, MID_A))
    weight = [occupied(v) for v in range(2)]
    dresses(0, 0)
    dresses(1, 0)
    each_half(sum_half, 0)
    wait_all((THIN, MID_A))
    release((MID_B,))
    lax.fori_loop(0, N, open_tail, 0)
    dresses(0, 2)
    dresses(1, 2)
    each_half(sum_half, 2)
    dresses(0, 1)
    wait_all((MID_B,))
    release((WIDE,))
    dresses(1, 1)
    each_half(sum_half, 1)
    prepare_late(near)
    lax.fori_loop(0, 2 * C, unpermute, 0)

    def along(k):
        each_half(sum_row, k)
        pass_on(NEAR, k, whole[0], 0)
        pass_on(PAIR, k, whole[0], 0)

    along(0)
    along(2)
    wait_last(0)
    dress_late(near)
    prepare_late(away)
    sum_half(LATE, near, late_whole)
    along(1)
    wait_last(1)
    send_far(0, whole[0], 0)
    send_far(2, whole[0], 0)
    dress_late(away, sum_block)
    send_far(1, whole[0], 0)
    sum_row(LATE, near, late_whole, [functools.partial(pass_on, NEAR, LATE)])
    unpermute_late(0)
    sum_row(LATE, away, halves, [functools.partial(pass_on, PAIR, LATE), functools.partial(send_far, LATE)])
    unpermute_late(1)
    for k in EARLY:
        sum_col(k, whole)
    sum_col(LATE, halves)
    for k in EARLY:
        take_final(k, whole)
    take_final(LATE, halves)
    for kind in range(5):
        bytes_of(every[kind], send.at[kind]).wait()
    bytes_of(amp_all.at[pl.ds(0, R - 1)], amp_sem.at[0]).wait()
    for k in EARLY + (LATE,):
        for h in range(B):
            bytes_of(of(GOT1, k).at[h], s1.at[k, h]).wait()
            bytes_of(of(GOT2, k).at[h, pl.ds(1, R - 1)], s2.at[k, h]).wait()

        @pl.when(jnp.logical_not(mine))
        def _():
            to_col(NEAR, k, near, all_of(k)[0], 0).wait_send()
            to_col(PAIR, k, away, all_of(k)[0], 0).wait_send()

        @pl.when(mine)
        def _():
            to_col(FAR, k, away, all_of(k)[0], 0).wait_send()
            for e in range(1, B):
                bytes_of(of(FINAL, k), s4.at[k]).wait()


def finish_kernel(mid, before, final, final_late, back, dressed, fock, natural, sem):
    pieces = sem.shape[0] - 1
    step = dressed.shape[1] // (pieces // 2)
    where = [(v, pl.ds(k * step, step)) for v in range(2) for k in range(pieces // 2)]
    stores = [pltpu.make_async_copy(before.at[w], dressed.at[w], sem.at[p]) for p, w in enumerate(where)]
    for store in stores:
        store.start()

    def place(value, k):
        hi = value.astype(bf16)
        lo = (value - hi.astype(f32)).astype(bf16)
        table = back[k * LANE : (k + 1) * LANE]
        return dot(hi, table) + dot(lo, table)

    packed = final_late[...]
    first = lax.broadcasted_iota(jnp.int32, packed.shape, 1) < mid
    upper = place(jnp.where(first, packed, 0.0), LATE)
    lower = place(jnp.where(first, 0.0, packed), LATE)
    value = jnp.concatenate([upper, lower[: natural.shape[0] - upper.shape[0]]], axis=0)
    for k in EARLY:
        value = value + place(final[k], k)
    natural[...] = value
    stores.append(pltpu.make_async_copy(natural, fock, sem.at[pieces]))
    stores[-1].start()
    for store in stores:
        store.wait()


def local(chol, amplitudes):
    B, R, C = lax.axis_size("pb"), lax.axis_size("row"), lax.axis_size("col")
    q_local, rw, cw = chol.shape
    n = cw // rw
    norb = C * cw
    occ = amplitudes.shape[0]
    groups = rw // SH
    mid = 64
    low = cw - 2 * LANE - mid
    rows = 2 * rw * low // LANE
    share = C // B
    N = R * C
    virtual = np.arange(groups * VG)
    widen = virtual[:, None] // VG * SH + OG + virtual[:, None] % VG == np.arange(rw)[None, :]
    index = np.arange(occ)
    place = np.arange(norb)[:, None] == (index // OG * SH + index % OG)[None, :]
    place = place.reshape(C, cw, occ)
    column = np.arange(cw)
    order = np.concatenate([column[column % SH < OG], column[column % SH >= OG]])
    perm = np.zeros((cw, 3 * LANE), bool)
    perm[order, np.arange(cw)] = True
    in_order = np.zeros((cw, 4 * LANE), bool)
    in_order[:, : 2 * LANE] = perm[:, : 2 * LANE]
    in_order[:, 2 * LANE : 2 * LANE + low] = perm[:, 2 * LANE + mid : 2 * LANE + mid + low]
    wide = perm[:, 2 * LANE : 2 * LANE + mid]
    in_order[:, 3 * LANE :] = np.concatenate([wide, wide], axis=1)
    late_columns = order[2 * LANE : 2 * LANE + mid]
    spans = []
    for j in range(C):
        start, stop = j * cw + late_columns.min(), j * cw + late_columns.max() + 1
        spans.append((int(start // LANE * LANE), int(min(-(-stop // LANE) * LANE, norb))))
    wide_back = np.zeros((C, 2, LANE, max(stop - start for start, stop in spans)), bool)
    for j, (start, stop) in enumerate(spans):
        for v in range(2):
            wide_back[j, v, v * mid + np.arange(mid), j * cw + late_columns - start] = True
    per_block = occ // C
    occ_of = np.zeros((C, LANE, occ), bool)
    for j in range(C):
        occ_of[j, np.arange(per_block), j * per_block + np.arange(per_block)] = True
    occ_of = occ_of.reshape(B, share * LANE, occ)
    late_rows = (rw // 2 + 7) // 8 * 8
    const = lambda array: jnp.asarray(array, bf16)
    hbm = pl.BlockSpec(memory_space=pl.ANY)
    vmem = pl.BlockSpec(memory_space=pltpu.VMEM)
    dma = pltpu.SemaphoreType.DMA
    half_width = lambda *shape: pltpu.VMEM(shape, bf16)
    full_width = lambda *shape: pltpu.VMEM(shape, f32)
    tables = [perm, widen, in_order, in_order.T, place, occ_of, wide_back]
    tables = [const(array) for array in tables]
    room = lambda array: half_width(*array.shape)
    before, final, final_late, back = pl.pallas_call(
        functools.partial(main_kernel, B, R, C, n, mid, low, rows, spans),
        out_shape=(
            pltpu.VMEM((2, norb, norb), bf16),
            pltpu.VMEM((3, rw, LANE), f32),
            pltpu.VMEM((late_rows, LANE), f32),
            pltpu.VMEM(tables[3].shape, bf16),
        ),
        in_specs=[hbm] * (2 + len(tables)),
        out_specs=(vmem, vmem, vmem, vmem),
        scratch_shapes=[
            half_width(SLOTS, 2, rw, cw),
            half_width(N, 2, 2, rw, LANE),
            half_width(N, rw, LANE),
            half_width(N, rows, LANE),
            half_width(C, R, rw, LANE),
            half_width(N, rows, LANE),
            half_width(2, 3, C, R, rw, LANE),
            full_width(C, C, cw, LANE),
            half_width(occ, rw),
            half_width(R, occ, rw),
            half_width(C, occ, cw),
            half_width(4, C, occ, LANE),
            half_width(2, C, cw, occ),
            half_width(2, occ, occ),
            full_width(cw, share * LANE),
            full_width(C, cw, share * LANE),
            half_width(3, B, share, R, rw, LANE),
            half_width(3, B, B - 1, R, rw, LANE),
            half_width(3, B, R, rw, LANE),
            half_width(3, B, R, rw, LANE),
            half_width(3, B, rw, LANE),
            half_width(3, 3, rw, LANE),
            half_width(B, share, R, late_rows, LANE),
            half_width(B, B - 1, R, late_rows, LANE),
            half_width(B, R, late_rows, LANE),
            half_width(B, R, late_rows, LANE),
            half_width(B, late_rows, LANE),
            half_width(3, late_rows, LANE),
            room(tables[0]),
            room(amplitudes),
            *[room(array) for i, array in enumerate(tables) if i not in (0, 3)],
            dma((5,)), dma((4,)), dma((B,)), dma((2,)), dma((SLOTS,)), dma((1 + len(tables),)),
            dma((4, B)), dma((4, B)), dma((C,)), dma((4, B)), dma((4, B, 2)), dma((4, 3)), dma((4, 3, 2)), dma((4,)),
            dma((4, 2)),
            *([half_width(2, 3, C, C, cw, LANE), half_width(C, C, cw, LANE)] if n > 1 else []),
        ],
        compiler_params=pltpu.CompilerParams(
            collective_id=0, has_side_effects=True, vmem_limit_bytes=MAIN_VMEM
        ),
        name="exchange",
    )(chol, amplitudes, *tables)
    return pl.pallas_call(
        functools.partial(finish_kernel, mid),
        out_shape=(
            jax.ShapeDtypeStruct((2, norb, norb), bf16),
            jax.ShapeDtypeStruct((rw, cw), f32),
        ),
        in_specs=[vmem] * 4,
        out_specs=(hbm, hbm),
        scratch_shapes=[full_width(rw, cw), dma((2 * C + 1,))],
        compiler_params=pltpu.CompilerParams(vmem_limit_bytes=16 * 1024 * 1024),
        name="finish",
    )(before, final, final_late, back)


def solution(mesh):
    return jax.shard_map(
        local,
        mesh=mesh,
        in_specs=(P("pb", "row", "col"), P(None, "row")),
        out_specs=(P(("pb", "row", "col"), None, None), P("row", "col")),
        check_vma=False,
    )
```

time: 183 us -> 180 us (0.984)
  Pallas kernels: 182 us -> 179 us
    pallas_call x2, Pallas kernels: 182 us -> 179 us  [the longest x1 176 us: local(): pl.pallas_call(functools.partial(main_kernel, B, R, C, n, mid, low, rows,...]
where the time goes in v5:
time: 180 us
  Pallas kernels  179 us (99%)
    pallas_call x1, Pallas kernels, local(): pl.pallas_call(functools.partial(main_kernel, B, R, C, n, mid, low, rows,...  176 us

profile of v5, /device:TPU:1, one launch (start us, length us, event | category | flops | bytes accessed | tf_op | source)
XLA Modules:
  0.0 179.7 jit_solution(18387963024761295650)
XLA Ops:
  0.6 175.8 %exchange.1 = (bf16[2,1344,1344]{2,1,0:T(8,128)(2,1)S(1)}, f32[3,336,128]{2,1,0:T(8,128)S(1)}, f32[168,128]{1,0:T(8,128)S(1)}, bf16[512,336]{1,0:T(8,128)(2,1)S(1)}) custom-call(bf16[32,336,336]{2,1,0:T(8,128)(2,1)} %chol.1, bf16[144,300]{1,0:T(8,128)(2,1)} %amp_in.1, bf16[336,384]{1,0:T(8,128)(2,1)} %constant.14.clone.perm_in, ...), custom_call_target="tpu_custom_call" | custom-call | tf_op jit(solution)/shard_map/exchange/pallas_call | solution.py:653
  176.4 3.3 %finish.1 = (bf16[2,1344,1344]{2,1,0:T(8,128)(2,1)}, f32[336,336]{1,0:T(8,128)}) custom-call(bf16[2,1344,1344]{2,1,0:T(8,128)(2,1)S(1)} %get-tuple-element.6.before, f32[3,336,128]{2,1,0:T(8,128)S(1)} %get-tuple-element.7.final, f32[168,128]{1,0:T(8,128)S(1)} %get-tuple-element.8.final_late, bf16[512,336]{1,0:T(8,128)(2,1)S(1)} %get-tuple-element.9.back), custom_call_target="tpu_custom_call" | custom-call | tf_op jit(solution)/shard_map/finish/pallas_call | solution.py:705
